TPU v7x, 16 devices: a 4x2x1 block of a 4x4x8 slice. The times are simulated.
16 devices in a mesh: dp: 2 (over y, z), tp: 8 (over x, core).
Axes of the slice: x: 4, y: 2, z: 1, core: 2. Of those that a mesh axis runs over, the one named last changes fastest.
The devices are a block of a 4x4x8 slice.
Arguments:
- x_in: bfloat16 [3072, 2048], P('dp'), parts along dimension 0
- g_norm: bfloat16 [2048], replicated
- w_q: bfloat16 [2048, 2048], P(None, 'tp')
- w_k: bfloat16 [2048, 1024], replicated
- w_v: bfloat16 [2048, 1024], replicated
- w_o: bfloat16 [2048, 2048], P('tp')
- w_gate: bfloat16 [2048, 6144], P(None, 'tp')
- w_up: bfloat16 [2048, 6144], P(None, 'tp')
- w_down: bfloat16 [6144, 2048], P('tp')
Outputs:
- output 1: bfloat16 [3072, 2048], P('dp'), parts along dimension 0
- output 2: bfloat16 [3072, 8, 128], P('dp', 'tp'), parts along dimension 0
- output 3: bfloat16 [3072, 8, 128], P('dp', 'tp'), parts along dimension 0
There are 2 independent parts. A program takes and returns all parts, laid end to end along the dimension named above; an argument that names none is the same for every part.
All inputs are finite; a program needn't handle non-finite values.
Results may differ from a plain program's by a relative error of at most 0.0121325.
Values are sent between devices in bfloat16 or wider.
A program may use at most 768 MiB of HBM per device.

v0:
```python
import math
import jax
import jax.numpy as jnp
from jax import lax
from jax.sharding import PartitionSpec as P

HEAD_DIM = 128
ROPE_BASE = 500000.0
NORM_EPS = 1e-5


def rope_tables(positions):
    inv_freq = ROPE_BASE ** (-jnp.arange(0, HEAD_DIM, 2, dtype=jnp.float32) / HEAD_DIM)
    angles = positions.astype(jnp.float32)[:, None] * inv_freq[None, :]
    return jnp.cos(angles), jnp.sin(angles)


def apply_rope(projected, cos_tab, sin_tab):
    half_dim = HEAD_DIM // 2
    lower_half = projected[..., :half_dim]
    upper_half = projected[..., half_dim:]
    cos_b = cos_tab[:, None, :]
    sin_b = sin_tab[:, None, :]
    return jnp.concatenate([lower_half * cos_b - upper_half * sin_b, upper_half * cos_b + lower_half * sin_b], axis=-1)


def rms_norm(x_rows, g_norm):
    x_f32 = x_rows.astype(jnp.float32)
    inv_rms = lax.rsqrt(jnp.mean(x_f32 * x_f32, axis=-1, keepdims=True) + NORM_EPS)
    return (x_f32 * inv_rms * g_norm.astype(jnp.float32)).astype(jnp.bfloat16)


def solution(mesh):
    tp_size = mesh.shape['tp']

    def local_layer(x_in, g_norm, w_q, w_k, w_v, w_o, w_gate, w_up, w_down):
        tokens, width = x_in.shape
        kv_heads = w_k.shape[1] // HEAD_DIM
        kv_local = max(kv_heads // tp_size, 1)
        q_local = w_q.shape[1] // HEAD_DIM
        group_size = q_local // kv_local
        q_block = min(128, tokens)
        score_scale = 1.0 / math.sqrt(HEAD_DIM)
        head_start = lax.axis_index('tp') * kv_heads // tp_size
        normed = rms_norm(x_in, g_norm)
        cos_tab, sin_tab = rope_tables(jnp.arange(tokens))
        w_k_mine = lax.dynamic_slice_in_dim(w_k, head_start * HEAD_DIM, kv_local * HEAD_DIM, axis=1)
        w_v_mine = lax.dynamic_slice_in_dim(w_v, head_start * HEAD_DIM, kv_local * HEAD_DIM, axis=1)
        k_proj = jnp.dot(normed, w_k_mine, preferred_element_type=jnp.float32).reshape(tokens, kv_local, HEAD_DIM)
        k_rot = apply_rope(k_proj, cos_tab, sin_tab).astype(jnp.bfloat16)
        v_proj = jnp.dot(normed, w_v_mine, preferred_element_type=jnp.float32).astype(jnp.bfloat16).reshape(tokens, kv_local, HEAD_DIM)
        key_pos = jnp.arange(tokens)

        def row_block(block_idx):
            row_start = block_idx * q_block
            normed_blk = lax.dynamic_slice_in_dim(normed, row_start, q_block, axis=0)
            cos_blk = lax.dynamic_slice_in_dim(cos_tab, row_start, q_block, axis=0)
            sin_blk = lax.dynamic_slice_in_dim(sin_tab, row_start, q_block, axis=0)
            q_proj = jnp.dot(normed_blk, w_q, preferred_element_type=jnp.float32).reshape(q_block, q_local, HEAD_DIM)
            q_rot = apply_rope(q_proj, cos_blk, sin_blk).astype(jnp.bfloat16).reshape(q_block, kv_local, group_size, HEAD_DIM)
            scores = jnp.einsum('qgrd,kgd->grqk', q_rot, k_rot, preferred_element_type=jnp.float32) * score_scale
            query_pos = row_start + jnp.arange(q_block)
            scores = jnp.where(key_pos[None, :] <= query_pos[:, None], scores, -1e30)
            probs_bf = jax.nn.softmax(scores, axis=-1).astype(jnp.bfloat16)
            attn_out = jnp.einsum('grqk,kgd->qgrd', probs_bf, v_proj, preferred_element_type=jnp.float32).astype(jnp.bfloat16).reshape(q_block, q_local * HEAD_DIM)
            gate_proj = jnp.dot(normed_blk, w_gate, preferred_element_type=jnp.float32)
            up_proj = jnp.dot(normed_blk, w_up, preferred_element_type=jnp.float32)
            hidden = (jax.nn.silu(gate_proj) * up_proj).astype(jnp.bfloat16)
            return (jnp.dot(attn_out, w_o, preferred_element_type=jnp.float32) + jnp.dot(hidden, w_down, preferred_element_type=jnp.float32)).astype(jnp.bfloat16)

        partial_sum = lax.map(row_block, jnp.arange(tokens // q_block)).reshape(tokens, width)
        reduced_sum = lax.psum(partial_sum, 'tp')
        y_out = (x_in.astype(jnp.float32) + reduced_sum.astype(jnp.float32)).astype(jnp.bfloat16)
        return y_out, k_rot, v_proj

    return jax.shard_map(local_layer, mesh=mesh, in_specs=(P('dp', None), P(None), P(None, 'tp'), P(None, None), P(None, None), P('tp', None), P(None, 'tp'), P(None, 'tp'), P('tp', None)), out_specs=(P('dp', None), P('dp', 'tp', None), P('dp', 'tp', None)), check_vma=False)
```

profile of v0, /device:TPU:113, one launch (start us, length us, event | category | flops | bytes accessed | tf_op | source)
XLA Modules:
  0.0 306.2 jit_solution(10202748137474242991)
XLA Ops:
  7.3 4.1 %fusion.33 = f32[1536]{0:T(1024)S(1)} fusion(bf16[1536,2048]{1,0:T(8,128)(2,1)} %param.11), kind=kLoop, calls=%fused_computation.45 | loop fusion | flops 9435648 | bytes 6297600 | tf_op jit(solution)/shard_map/reduce_sum | solution.py:29
  11.4 4.3 %fusion.35 = bf16[1536,2048]{1,0:T(8,128)(2,1)S(1)} fusion(bf16[1536,2048]{1,0:T(8,128)(2,1)} %param.11, f32[2048]{0:T(1024)S(1)} %convert_element_type.70, f32[1536]{0:T(1024)S(1)} %add_rsqrt_fusion), kind=kLoop, calls=%fused_computation.47 | loop fusion | flops 12582912 | bytes 12597248 | tf_op jit(solution)/shard_map/convert_element_type | solution.py:30
  15.7 5.0 %multiply_sine_fusion = (f32[1536,64]{1,0:T(8,128)}, f32[1536,64]{1,0:T(8,128)}) fusion(f32[64]{0:T(128)S(1)} %multiply_power_fusion, f32[1536]{0:T(1024)S(1)} %iota_convert_fusion), kind=kLoop, calls=%fused_computation.52 | loop fusion | flops 98304 | bytes 792832 | tf_op jit(solution)/shard_map/sin | solution.py:15
  20.8 3.3 %convolution_bitcast_fusion = f32[1536,1,128]{0,2,1:T(8,128)S(1)} fusion(bf16[1536,2048]{1,0:T(8,128)(2,1)S(1)} %fusion.35, bf16[2048,1024]{1,0:T(8,128)(2,1)} %param.14, s32[]{:T(128)S(6)} %select_n.19), kind=kOutput, calls=%fused_computation.49 | convolution fusion | flops 805306368 | bytes 7602180 | tf_op jit(solution)/shard_map/dot_general | solution.py:49
  24.1 1.6 fusion.45
  26.7 4.7 %fusion.37 = bf16[1536,1,128]{2,0,1:T(8,128)(2,1)S(1)} fusion(bf16[1536,2048]{1,0:T(8,128)(2,1)} %copy-done, bf16[2048,1024]{1,0:T(8,128)(2,1)} %param.15, s32[]{:T(128)S(6)} %select_n.19), kind=kOutput, calls=%fused_computation.51 | convolution fusion | flops 805502976 | bytes 7208964 | tf_op jit(solution)/shard_map/dot_general | solution.py:51
  32.3 177.3 %while.11 = (s32[]{:T(128)}, bf16[12,128,2048]{2,1,0:T(8,128)(2,1)}, s32[12]{0:T(128)S(1)}, bf16[1536,2048]{1,0:T(8,128)(2,1)}, bf16[2048,256]{1,0:T(8,128)(2,1)...) while((s32[]{:T(128)}, ...), condition=%wide.region_4.5_spmd.clone, body=%wide.region_1.4_spmd.clone.sunk | while | flops 1682472576 | bytes 36248328 | solution.py:71
  36.4 1.7 fusion.92
  38.5 1.5 convolution_convert_fusion.3
  40.4 1.6 fusion.95
  42.0 5.1 %fusion.96 = bf16[12,128,2048]{2,1,0:T(8,128)(2,1)} fusion(bf16[12,128,2048]{2,1,0:T(8,128)(2,1)} %get-tuple-element.271, s32[]{:T(128)} %get-tuple-element.270, f32[128,2048]{1,0:T(8,128)S(1)} %fusion.94, bf16[768,2048]{1,0:T(8,128)(2,1)} %get-tuple-element.299, bf16[2048,768]{1,0:T(8,128)(2,1)} %get-tuple-element.298, ...), kind=kOutput, calls=%fused_computation.7.clone.1 | convolution fusion | flops 806420480 | bytes 8782340 | tf_op jit(solution)/shard_map/while/body/eval_jaxpr/dot_general | solution.py:69
  48.4 1.4 fusion.90
  51.2 1.7 fusion.92
  53.3 1.5 convolution_convert_fusion.3
  55.2 1.6 fusion.95
  56.8 5.1 %fusion.96 = bf16[12,128,2048]{2,1,0:T(8,128)(2,1)} fusion(bf16[12,128,2048]{2,1,0:T(8,128)(2,1)} %get-tuple-element.271, s32[]{:T(128)} %get-tuple-element.270, f32[128,2048]{1,0:T(8,128)S(1)} %fusion.94, bf16[768,2048]{1,0:T(8,128)(2,1)} %get-tuple-element.299, bf16[2048,768]{1,0:T(8,128)(2,1)} %get-tuple-element.298, ...), kind=kOutput, calls=%fused_computation.7.clone.1 | convolution fusion | flops 806420480 | bytes 8782340 | tf_op jit(solution)/shard_map/while/body/eval_jaxpr/dot_general | solution.py:69
  63.2 1.4 fusion.90
  66.0 1.7 fusion.92
  68.1 1.5 convolution_convert_fusion.3
  69.9 1.6 fusion.95
  71.6 5.1 %fusion.96 = bf16[12,128,2048]{2,1,0:T(8,128)(2,1)} fusion(bf16[12,128,2048]{2,1,0:T(8,128)(2,1)} %get-tuple-element.271, s32[]{:T(128)} %get-tuple-element.270, f32[128,2048]{1,0:T(8,128)S(1)} %fusion.94, bf16[768,2048]{1,0:T(8,128)(2,1)} %get-tuple-element.299, bf16[2048,768]{1,0:T(8,128)(2,1)} %get-tuple-element.298, ...), kind=kOutput, calls=%fused_computation.7.clone.1 | convolution fusion | flops 806420480 | bytes 8782340 | tf_op jit(solution)/shard_map/while/body/eval_jaxpr/dot_general | solution.py:69
  78.0 1.4 fusion.90
  80.8 1.7 fusion.92
  82.8 1.5 convolution_convert_fusion.3
  84.7 1.6 fusion.95
  86.3 5.1 %fusion.96 = bf16[12,128,2048]{2,1,0:T(8,128)(2,1)} fusion(bf16[12,128,2048]{2,1,0:T(8,128)(2,1)} %get-tuple-element.271, s32[]{:T(128)} %get-tuple-element.270, f32[128,2048]{1,0:T(8,128)S(1)} %fusion.94, bf16[768,2048]{1,0:T(8,128)(2,1)} %get-tuple-element.299, bf16[2048,768]{1,0:T(8,128)(2,1)} %get-tuple-element.298, ...), kind=kOutput, calls=%fused_computation.7.clone.1 | convolution fusion | flops 806420480 | bytes 8782340 | tf_op jit(solution)/shard_map/while/body/eval_jaxpr/dot_general | solution.py:69
  92.7 1.4 fusion.90
  95.5 1.7 fusion.92
  97.6 1.5 convolution_convert_fusion.3
  99.5 1.6 fusion.95
  101.1 5.1 %fusion.96 = bf16[12,128,2048]{2,1,0:T(8,128)(2,1)} fusion(bf16[12,128,2048]{2,1,0:T(8,128)(2,1)} %get-tuple-element.271, s32[]{:T(128)} %get-tuple-element.270, f32[128,2048]{1,0:T(8,128)S(1)} %fusion.94, bf16[768,2048]{1,0:T(8,128)(2,1)} %get-tuple-element.299, bf16[2048,768]{1,0:T(8,128)(2,1)} %get-tuple-element.298, ...), kind=kOutput, calls=%fused_computation.7.clone.1 | convolution fusion | flops 806420480 | bytes 8782340 | tf_op jit(solution)/shard_map/while/body/eval_jaxpr/dot_general | solution.py:69
  107.5 1.4 fusion.90
  110.3 1.7 fusion.92
  112.4 1.5 convolution_convert_fusion.3
  114.2 1.6 fusion.95
  115.9 5.1 %fusion.96 = bf16[12,128,2048]{2,1,0:T(8,128)(2,1)} fusion(bf16[12,128,2048]{2,1,0:T(8,128)(2,1)} %get-tuple-element.271, s32[]{:T(128)} %get-tuple-element.270, f32[128,2048]{1,0:T(8,128)S(1)} %fusion.94, bf16[768,2048]{1,0:T(8,128)(2,1)} %get-tuple-element.299, bf16[2048,768]{1,0:T(8,128)(2,1)} %get-tuple-element.298, ...), kind=kOutput, calls=%fused_computation.7.clone.1 | convolution fusion | flops 806420480 | bytes 8782340 | tf_op jit(solution)/shard_map/while/body/eval_jaxpr/dot_general | solution.py:69
  122.3 1.4 fusion.90
  125.1 1.7 fusion.92
  127.1 1.5 convolution_convert_fusion.3
  129.0 1.6 fusion.95
  130.6 5.1 %fusion.96 = bf16[12,128,2048]{2,1,0:T(8,128)(2,1)} fusion(bf16[12,128,2048]{2,1,0:T(8,128)(2,1)} %get-tuple-element.271, s32[]{:T(128)} %get-tuple-element.270, f32[128,2048]{1,0:T(8,128)S(1)} %fusion.94, bf16[768,2048]{1,0:T(8,128)(2,1)} %get-tuple-element.299, bf16[2048,768]{1,0:T(8,128)(2,1)} %get-tuple-element.298, ...), kind=kOutput, calls=%fused_computation.7.clone.1 | convolution fusion | flops 806420480 | bytes 8782340 | tf_op jit(solution)/shard_map/while/body/eval_jaxpr/dot_general | solution.py:69
  137.0 1.4 fusion.90
  139.8 1.7 fusion.92
  141.9 1.5 convolution_convert_fusion.3
  143.8 1.6 fusion.95
  145.4 5.1 %fusion.96 = bf16[12,128,2048]{2,1,0:T(8,128)(2,1)} fusion(bf16[12,128,2048]{2,1,0:T(8,128)(2,1)} %get-tuple-element.271, s32[]{:T(128)} %get-tuple-element.270, f32[128,2048]{1,0:T(8,128)S(1)} %fusion.94, bf16[768,2048]{1,0:T(8,128)(2,1)} %get-tuple-element.299, bf16[2048,768]{1,0:T(8,128)(2,1)} %get-tuple-element.298, ...), kind=kOutput, calls=%fused_computation.7.clone.1 | convolution fusion | flops 806420480 | bytes 8782340 | tf_op jit(solution)/shard_map/while/body/eval_jaxpr/dot_general | solution.py:69
  154.6 1.7 fusion.92
  156.7 1.5 convolution_convert_fusion.3
  158.5 1.6 fusion.95
  160.2 5.1 %fusion.96 = bf16[12,128,2048]{2,1,0:T(8,128)(2,1)} fusion(bf16[12,128,2048]{2,1,0:T(8,128)(2,1)} %get-tuple-element.271, s32[]{:T(128)} %get-tuple-element.270, f32[128,2048]{1,0:T(8,128)S(1)} %fusion.94, bf16[768,2048]{1,0:T(8,128)(2,1)} %get-tuple-element.299, bf16[2048,768]{1,0:T(8,128)(2,1)} %get-tuple-element.298, ...), kind=kOutput, calls=%fused_computation.7.clone.1 | convolution fusion | flops 806420480 | bytes 8782340 | tf_op jit(solution)/shard_map/while/body/eval_jaxpr/dot_general | solution.py:69
  169.4 1.7 fusion.92
  171.5 1.5 convolution_convert_fusion.3
  173.3 1.6 fusion.95
  174.9 5.1 %fusion.96 = bf16[12,128,2048]{2,1,0:T(8,128)(2,1)} fusion(bf16[12,128,2048]{2,1,0:T(8,128)(2,1)} %get-tuple-element.271, s32[]{:T(128)} %get-tuple-element.270, f32[128,2048]{1,0:T(8,128)S(1)} %fusion.94, bf16[768,2048]{1,0:T(8,128)(2,1)} %get-tuple-element.299, bf16[2048,768]{1,0:T(8,128)(2,1)} %get-tuple-element.298, ...), kind=kOutput, calls=%fused_computation.7.clone.1 | convolution fusion | flops 806420480 | bytes 8782340 | tf_op jit(solution)/shard_map/while/body/eval_jaxpr/dot_general | solution.py:69
  184.1 1.7 fusion.92
  186.2 1.5 convolution_convert_fusion.3
  188.1 1.6 fusion.95
  189.7 5.1 %fusion.96 = bf16[12,128,2048]{2,1,0:T(8,128)(2,1)} fusion(bf16[12,128,2048]{2,1,0:T(8,128)(2,1)} %get-tuple-element.271, s32[]{:T(128)} %get-tuple-element.270, f32[128,2048]{1,0:T(8,128)S(1)} %fusion.94, bf16[768,2048]{1,0:T(8,128)(2,1)} %get-tuple-element.299, bf16[2048,768]{1,0:T(8,128)(2,1)} %get-tuple-element.298, ...), kind=kOutput, calls=%fused_computation.7.clone.1 | convolution fusion | flops 806420480 | bytes 8782340 | tf_op jit(solution)/shard_map/while/body/eval_jaxpr/dot_general | solution.py:69
  198.9 1.7 fusion.92
  201.0 1.5 convolution_convert_fusion.3
  202.9 1.6 fusion.95
  204.5 5.1 %fusion.96 = bf16[12,128,2048]{2,1,0:T(8,128)(2,1)} fusion(bf16[12,128,2048]{2,1,0:T(8,128)(2,1)} %get-tuple-element.271, s32[]{:T(128)} %get-tuple-element.270, f32[128,2048]{1,0:T(8,128)S(1)} %fusion.94, bf16[768,2048]{1,0:T(8,128)(2,1)} %get-tuple-element.299, bf16[2048,768]{1,0:T(8,128)(2,1)} %get-tuple-element.298, ...), kind=kOutput, calls=%fused_computation.7.clone.1 | convolution fusion | flops 806420480 | bytes 8782340 | tf_op jit(solution)/shard_map/while/body/eval_jaxpr/dot_general | solution.py:69
  209.6 78.7 %all-reduce.2.cloned.1.call-done = bf16[1536,2048]{1,0:T(8,128)(2,1)} async-done(((bf16[1536,2048]{1,0:T(8,128)(2,1)}), bf16[1536,2048]{1,0:T(8,128)(2,1)}) %all-reduce.2.cloned.1.call-update) | async-done | bytes 6291472 | tf_op jit(solution)/shard_map/psum | solution.py:72
  288.3 11.0 %fusion.36 = bf16[1536,2048]{1,0:T(8,128)(2,1)} fusion(bf16[1536,2048]{1,0:T(8,128)(2,1)} %param.11, bf16[1536,2048]{1,0:T(8,128)(2,1)} %all-reduce.2.cloned.1.call-done), kind=kLoop, calls=%fused_computation.48 | loop fusion | flops 12582912 | bytes 18874368 | tf_op jit(solution)/shard_map/convert_element_type | solution.py:73
  (158 shorter events, 41.7 us)
Async XLA Ops:
  7.2 4.2 %copy-start.5 = (bf16[2048]{0:T(1024)(128)(2,1)S(1)}, bf16[2048]{0:T(1024)(128)(2,1)}, u32[]{:S(2)}) copy-start(bf16[2048]{0:T(1024)(128)(2,1)} %param.12) | copy-start | bytes 12292
  7.2 281.1 %all-reduce.2.cloned.1.call-start = ((), (), s32[]{:S(2)}) async-start(), calls=%async_computation | async-start | bytes 12582912 | tf_op jit(solution)/shard_map/psum | solution.py:72
  15.7 10.0 %copy-start = (bf16[1536,2048]{1,0:T(8,128)(2,1)}, bf16[1536,2048]{1,0:T(8,128)(2,1)S(1)}, u32[]{:S(2)}) copy-start(bf16[1536,2048]{1,0:T(8,128)(2,1)S(1)} %fusion.35) | copy-start | bytes 18874372
  24.0 8.3 %copy-start.2 = (bf16[2048,256]{1,0:T(8,128)(2,1)S(1)}, bf16[2048,256]{1,0:T(8,128)(2,1)}, u32[]{:S(2)}) copy-start(bf16[2048,256]{1,0:T(8,128)(2,1)} %param.13) | copy-start | bytes 3145732
  24.0 8.2 %copy-start.3 = (bf16[256,2048]{1,0:T(8,128)(2,1)S(1)}, bf16[256,2048]{1,0:T(8,128)(2,1)}, u32[]{:S(2)}) copy-start(bf16[256,2048]{1,0:T(8,128)(2,1)} %param.16) | copy-start | bytes 3145732
  31.3 1.0 copy-start.4
  36.4 3.9 %copy-start.1 = (bf16[2048,768]{1,0:T(8,128)(2,1)S(1)}, bf16[2048,768]{1,0:T(8,128)(2,1)}, u32[]{:S(2)}) copy-start(bf16[2048,768]{1,0:T(8,128)(2,1)} %get-tuple-element.297) | copy-start | bytes 9437188 | tf_op jit(solution)/shard_map/while
  51.2 3.9 %copy-start.1 = (bf16[2048,768]{1,0:T(8,128)(2,1)S(1)}, bf16[2048,768]{1,0:T(8,128)(2,1)}, u32[]{:S(2)}) copy-start(bf16[2048,768]{1,0:T(8,128)(2,1)} %get-tuple-element.297) | copy-start | bytes 9437188 | tf_op jit(solution)/shard_map/while
  66.0 3.9 %copy-start.1 = (bf16[2048,768]{1,0:T(8,128)(2,1)S(1)}, bf16[2048,768]{1,0:T(8,128)(2,1)}, u32[]{:S(2)}) copy-start(bf16[2048,768]{1,0:T(8,128)(2,1)} %get-tuple-element.297) | copy-start | bytes 9437188 | tf_op jit(solution)/shard_map/while
  80.7 3.9 %copy-start.1 = (bf16[2048,768]{1,0:T(8,128)(2,1)S(1)}, bf16[2048,768]{1,0:T(8,128)(2,1)}, u32[]{:S(2)}) copy-start(bf16[2048,768]{1,0:T(8,128)(2,1)} %get-tuple-element.297) | copy-start | bytes 9437188 | tf_op jit(solution)/shard_map/while
  95.5 3.9 %copy-start.1 = (bf16[2048,768]{1,0:T(8,128)(2,1)S(1)}, bf16[2048,768]{1,0:T(8,128)(2,1)}, u32[]{:S(2)}) copy-start(bf16[2048,768]{1,0:T(8,128)(2,1)} %get-tuple-element.297) | copy-start | bytes 9437188 | tf_op jit(solution)/shard_map/while
  110.3 3.9 %copy-start.1 = (bf16[2048,768]{1,0:T(8,128)(2,1)S(1)}, bf16[2048,768]{1,0:T(8,128)(2,1)}, u32[]{:S(2)}) copy-start(bf16[2048,768]{1,0:T(8,128)(2,1)} %get-tuple-element.297) | copy-start | bytes 9437188 | tf_op jit(solution)/shard_map/while
  125.1 3.9 %copy-start.1 = (bf16[2048,768]{1,0:T(8,128)(2,1)S(1)}, bf16[2048,768]{1,0:T(8,128)(2,1)}, u32[]{:S(2)}) copy-start(bf16[2048,768]{1,0:T(8,128)(2,1)} %get-tuple-element.297) | copy-start | bytes 9437188 | tf_op jit(solution)/shard_map/while
  139.8 3.9 %copy-start.1 = (bf16[2048,768]{1,0:T(8,128)(2,1)S(1)}, bf16[2048,768]{1,0:T(8,128)(2,1)}, u32[]{:S(2)}) copy-start(bf16[2048,768]{1,0:T(8,128)(2,1)} %get-tuple-element.297) | copy-start | bytes 9437188 | tf_op jit(solution)/shard_map/while
  154.6 3.9 %copy-start.1 = (bf16[2048,768]{1,0:T(8,128)(2,1)S(1)}, bf16[2048,768]{1,0:T(8,128)(2,1)}, u32[]{:S(2)}) copy-start(bf16[2048,768]{1,0:T(8,128)(2,1)} %get-tuple-element.297) | copy-start | bytes 9437188 | tf_op jit(solution)/shard_map/while
  169.4 3.9 %copy-start.1 = (bf16[2048,768]{1,0:T(8,128)(2,1)S(1)}, bf16[2048,768]{1,0:T(8,128)(2,1)}, u32[]{:S(2)}) copy-start(bf16[2048,768]{1,0:T(8,128)(2,1)} %get-tuple-element.297) | copy-start | bytes 9437188 | tf_op jit(solution)/shard_map/while
  184.1 3.9 %copy-start.1 = (bf16[2048,768]{1,0:T(8,128)(2,1)S(1)}, bf16[2048,768]{1,0:T(8,128)(2,1)}, u32[]{:S(2)}) copy-start(bf16[2048,768]{1,0:T(8,128)(2,1)} %get-tuple-element.297) | copy-start | bytes 9437188 | tf_op jit(solution)/shard_map/while
  198.9 3.9 %copy-start.1 = (bf16[2048,768]{1,0:T(8,128)(2,1)S(1)}, bf16[2048,768]{1,0:T(8,128)(2,1)}, u32[]{:S(2)}) copy-start(bf16[2048,768]{1,0:T(8,128)(2,1)} %get-tuple-element.297) | copy-start | bytes 9437188 | tf_op jit(solution)/shard_map/while
Sparse Core Ops, SparseCore 0:
  209.7 78.5 all-reduce.1
where the time goes:
time: 309 us; the launch traced here: 306 us
  matrix products  147 us (48%)
  waiting for transfers between devices  78.8 us (26%)
  other arithmetic  33.2 us (11%)
  local copies, waits for them, and re-layouts  23.7 us (8%)
  between operations  14.2 us (5%)
  loops' own time  9.18 us (3%)
    psum x1, waiting for transfers between devices, local_layer(): reduced_sum = lax.psum(partial_sum, 'tp')  78.7 us
    dot_general x12, matrix products, row_block(): jnp.dot(hidden, w_down, preferred_element_type=jnp.float32)  60.9 us
    dot_general x12, matrix products, row_block(): jnp.einsum('qgrd,kgd->grqk', q_rot, k_rot, preferred_element_type=jnp.flo...  20.6 us
    dot_general x12, matrix products, row_block(): gate_proj = jnp.dot(normed_blk, w_gate, preferred_element_type=jnp.float32)  19.5 us
    dot_general x12, matrix products, row_block(): jnp.einsum('grqk,kgd->qgrd', probs_bf, v_proj, preferred_element_type=jnp...  18.1 us
    dot_general x12, matrix products, row_block(): jnp.dot(normed_blk, w_q, preferred_element_type=jnp.float32)  16.3 us
    convert_element_type x1, other arithmetic, local_layer(): (x_in.astype(jnp.float32) + reduced_sum.astype(jnp.float32)).astype(jnp.b...  11 us
    dynamic_slice x12, local copies, waits for them, and re-layouts, row_block(): sin_blk = lax.dynamic_slice_in_dim(sin_tab, row_start, q_block, axis=0)  10.6 us
  transfers between devices with their start and end apart: 1, of which 1 were waited for; matrix products, arithmetic and copies ran while one was open for 0% of the time, Pallas kernels for 0%

commit v1 on v0

v1 whole, which is shorter than its diff:
```python
import functools
import math
import numpy as np
import jax
import jax.numpy as jnp
from jax import lax
from jax.experimental import pallas as pl
from jax.experimental.pallas import tpu as pltpu
from jax.sharding import PartitionSpec as P

HEAD_DIM = 128
ROPE_BASE = 500000.0
NORM_EPS = 1e-5
ROWS = 256
KEYS = 256
TILE = 256
F32 = jnp.float32
BF16 = jnp.bfloat16
MESH = pl.DeviceIdType.MESH

(SWAP, FWD_R, OWN_R, FWD_L, OWN_L, SUM_R, SUM_L, OUT_R, OUT_L, OUT_P, FAR_R, FAR_L,
 P_LEFT, P_RIGHT, P_FAR_A, P_FAR_B) = range(16)
N_KINDS = 16


def rope_constants(rows, blocks):
    inv_freq = ROPE_BASE ** (-np.arange(0, HEAD_DIM, 2, dtype=np.float64) / HEAD_DIM)
    def tables(positions):
        ang = positions[:, None] * inv_freq[None, :]
        cos, sin = np.cos(ang), np.sin(ang)
        return (np.concatenate([cos, cos], 1).astype(np.float32),
                np.concatenate([-sin, sin], 1).astype(np.float32))
    cos_r, sin_r = tables(np.arange(rows, dtype=np.float64))
    cos_t, sin_t = tables(np.arange(blocks, dtype=np.float64) * rows)
    return cos_r, sin_r, cos_t, sin_t


def layer_kernel(n_tp, x_hbm, g_ref, wq_hbm, wk_hbm, wv_hbm, wo_hbm, wg_hbm, wu_hbm, wd_hbm,
                 cos_r, sin_r, cos_t, sin_t, y_ref, k_ref, v_ref,
                 x_v, wqkv, wgu, wod, a_s, q_s, s_s, m_s, l_s, o_s, om_s, part, swap, fwd, from_l, from_r,
                 load_sem, send_sem, recv_sem):
    tokens, width = x_v.shape
    blocks = tokens // ROWS
    half = ROWS // 2
    n_chip = n_tp // 2
    chunk = half // n_chip
    wh = width // 2
    qw = wq_hbm.shape[1]
    heads = qw // HEAD_DIM
    ff = wg_hbm.shape[1]
    me = lax.axis_index('tp')
    chip, core = me // 2, lax.rem(me, 2)
    partner = chip * 2 + 1 - core
    c_r = lax.rem(chip + 1, n_chip)
    c_l = lax.rem(chip + n_chip - 1, n_chip)
    c_o = lax.rem(chip + 2, n_chip)
    right = c_r * 2 + core
    left = c_l * 2 + core

    kv_col = pl.multiple_of(me * HEAD_DIM, HEAD_DIM)
    def x_load(t):
        rows = pl.ds(pl.multiple_of(t * ROWS, ROWS), ROWS)
        return pltpu.make_async_copy(x_hbm.at[rows], x_v.at[rows], load_sem.at[8 + t])
    w_loads = [
        pltpu.make_async_copy(wq_hbm, wqkv.at[:, pl.ds(0, qw)], load_sem.at[0]),
        pltpu.make_async_copy(wk_hbm.at[:, pl.ds(kv_col, HEAD_DIM)], wqkv.at[:, pl.ds(qw, HEAD_DIM)], load_sem.at[1]),
        pltpu.make_async_copy(wv_hbm.at[:, pl.ds(kv_col, HEAD_DIM)], wqkv.at[:, pl.ds(qw + HEAD_DIM, HEAD_DIM)], load_sem.at[2]),
        pltpu.make_async_copy(wg_hbm, wgu.at[:, pl.ds(0, ff)], load_sem.at[3]),
        pltpu.make_async_copy(wu_hbm, wgu.at[:, pl.ds(ff, ff)], load_sem.at[4]),
        pltpu.make_async_copy(wo_hbm, wod.at[pl.ds(0, qw)], load_sem.at[5]),
        pltpu.make_async_copy(wd_hbm, wod.at[pl.ds(qw, ff)], load_sem.at[6]),
    ]
    x_load(0).start()
    for cp in w_loads:
        cp.start()
    for t in range(1, blocks):
        x_load(t).start()

    barrier = pltpu.get_barrier_semaphore()
    for dev in (partner, left, right):
        pl.semaphore_signal(barrier, inc=1, device_id={'tp': dev}, device_id_type=MESH)
    k_ref[...] = jnp.zeros_like(k_ref)
    v_ref[...] = jnp.zeros_like(v_ref)
    pl.semaphore_wait(barrier, 3)

    def rows_of(t, c):
        return pl.ds(pl.multiple_of(t * ROWS + core * half + c * chunk, chunk), chunk)

    def slot(t):
        return pl.ds(pl.multiple_of(t * chunk, chunk), chunk)

    A, B = pl.ds(0, wh), pl.ds(wh, wh)

    def copy(kind, t):
        other = pl.ds(pl.multiple_of(t * ROWS + (1 - core) * half, half), half)
        src, dst, dev = {
            SWAP: lambda: (part.at[other], swap.at[pl.ds(pl.multiple_of(t * half, half), half)], partner),
            FWD_R: lambda: (part.at[rows_of(t, c_o), A], fwd.at[slot(t), A], right),
            OWN_R: lambda: (part.at[rows_of(t, c_r), B], from_l.at[slot(t), B], right),
            FWD_L: lambda: (part.at[rows_of(t, c_o), B], fwd.at[slot(t), B], left),
            OWN_L: lambda: (part.at[rows_of(t, c_l), A], from_r.at[slot(t), A], left),
            SUM_R: lambda: (part.at[rows_of(t, c_r), A], from_l.at[slot(t), A], right),
            SUM_L: lambda: (part.at[rows_of(t, c_l), B], from_r.at[slot(t), B], left),
            OUT_R: lambda: (y_ref.at[rows_of(t, chip)], y_ref.at[rows_of(t, chip)], right),
            OUT_L: lambda: (y_ref.at[rows_of(t, chip)], y_ref.at[rows_of(t, chip)], left),
            OUT_P: lambda: (y_ref.at[rows_of(t, chip)], y_ref.at[rows_of(t, chip)], partner),
            FAR_R: lambda: (y_ref.at[rows_of(t, c_l), A], y_ref.at[rows_of(t, c_l), A], right),
            FAR_L: lambda: (y_ref.at[rows_of(t, c_r), B], y_ref.at[rows_of(t, c_r), B], left),
            P_LEFT: lambda: (y_ref.at[rows_of(t, c_l)], y_ref.at[rows_of(t, c_l)], partner),
            P_RIGHT: lambda: (y_ref.at[rows_of(t, c_r)], y_ref.at[rows_of(t, c_r)], partner),
            P_FAR_A: lambda: (y_ref.at[rows_of(t, c_o), A], y_ref.at[rows_of(t, c_o), A], partner),
            P_FAR_B: lambda: (y_ref.at[rows_of(t, c_o), B], y_ref.at[rows_of(t, c_o), B], partner),
        }[kind]()
        return pltpu.make_async_remote_copy(
            src_ref=src, dst_ref=dst, send_sem=send_sem.at[kind, t], recv_sem=recv_sem.at[kind, t],
            device_id={'tp': dev}, device_id_type=MESH)

    scale = 1.0 / math.sqrt(HEAD_DIM) * math.log2(math.e)

    def project(t):
        x_load(t).wait()
        step = 64
        for i in range(ROWS // step):
            xf = x_v[pl.ds(pl.multiple_of(t * ROWS + i * step, step), step), :].astype(F32)
            inv = lax.rsqrt(jnp.mean(xf * xf, axis=-1, keepdims=True) + NORM_EPS)
            a_s[pl.ds(i * step, step), :] = (xf * inv * g_ref[...].astype(F32)).astype(BF16)

        @pl.when(t == 0)
        def _():
            for cp in w_loads[:3]:
                cp.wait()
        a = a_s[...]
        c0, s0 = cos_t[pl.ds(t, 1), :], sin_t[pl.ds(t, 1), :]
        cos = cos_r[...] * c0 - sin_r[...] * s0
        sin = sin_r[...] * c0 + cos_r[...] * s0
        rot = lambda p: (p * cos + pltpu.roll(p, HEAD_DIM // 2, 1) * sin).astype(BF16)
        q = jnp.dot(a, wqkv[:, pl.ds(0, qw)], preferred_element_type=F32)
        kv = jnp.dot(a, wqkv[:, pl.ds(qw, 2 * HEAD_DIM)], preferred_element_type=F32)
        for h in range(heads):
            q_s[pl.ds(h * ROWS, ROWS), :] = rot(q[:, h * HEAD_DIM:(h + 1) * HEAD_DIM])
        rows = pl.ds(pl.multiple_of(t * ROWS, ROWS), ROWS)
        k_ref[rows, :] = rot(kv[:, :HEAD_DIM])
        v_ref[rows, :] = kv[:, HEAD_DIM:].astype(BF16)

    def lanes(op, s):
        acc = s[:, :128]
        for i in range(1, KEYS // 128):
            acc = op(acc, s[:, i * 128:(i + 1) * 128])
        return acc

    def attend(t):
        last = (t * ROWS) // KEYS

        def keys(kb):
            return pl.ds(pl.multiple_of(kb * KEYS, KEYS), KEYS)

        def score(kb):
            return lax.dot_general(q_s[...], k_ref[keys(kb), :], (((1,), (1,)), ((), ())), preferred_element_type=F32)

        s = score(last)
        shape = (heads, ROWS, KEYS)
        q_pos = t * ROWS + lax.broadcasted_iota(jnp.int32, shape, 1).reshape(heads * ROWS, KEYS)
        k_pos = last * KEYS + lax.broadcasted_iota(jnp.int32, shape, 2).reshape(heads * ROWS, KEYS)
        s = jnp.where(k_pos <= q_pos, s, -1e30)
        s_s[last] = s
        m_s[...] = lanes(jnp.maximum, s)

        def pass1(kb, _):
            s = score(kb)
            s_s[kb] = s
            m_s[...] = jnp.maximum(m_s[...], lanes(jnp.maximum, s))
            return 0
        lax.fori_loop(0, last, pass1, 0)
        m_s[...] = jnp.broadcast_to(jnp.max(m_s[...], axis=-1, keepdims=True) * scale, m_s.shape)
        l_s[...] = jnp.zeros_like(l_s)

        def pass2(kb, _):
            m = m_s[...]
            p = jnp.exp2(s_s[kb] * scale - jnp.concatenate([m] * (KEYS // 128), axis=1))
            s_s[kb] = p
            l_s[...] += lanes(jnp.add, p)
            return 0
        lax.fori_loop(0, last + 1, pass2, 0)
        l_s[...] = jnp.broadcast_to(1.0 / jnp.sum(l_s[...], axis=-1, keepdims=True), l_s.shape)
        o_s[...] = jnp.zeros_like(o_s)

        def pass3(kb, _):
            r = l_s[...]
            p = (s_s[kb] * jnp.concatenate([r] * (KEYS // 128), axis=1)).astype(BF16)
            o_s[...] += jnp.dot(p, v_ref[keys(kb), :], preferred_element_type=F32)
            return 0
        lax.fori_loop(0, last + 1, pass3, 0)
        for h in range(heads):
            om_s[:, pl.ds(h * HEAD_DIM, HEAD_DIM)] = o_s[pl.ds(h * ROWS, ROWS), :].astype(BF16)

    def mlp(t):
        @pl.when(t == 0)
        def _():
            for cp in w_loads[3:5]:
                cp.wait()
        a = a_s[...]
        for j in range(ff // TILE):
            gate = jnp.dot(a, wgu[:, pl.ds(j * TILE, TILE)], preferred_element_type=F32)
            up = jnp.dot(a, wgu[:, pl.ds(ff + j * TILE, TILE)], preferred_element_type=F32)
            om_s[:, pl.ds(qw + j * TILE, TILE)] = (jax.nn.silu(gate) * up).astype(BF16)

    def out_half(t, which):
        row0 = pl.multiple_of(which * half, half)
        om = om_s[pl.ds(row0, half), :]
        rows = pl.ds(pl.multiple_of(t * ROWS + which * half, half), half)
        for j in range(width // TILE):
            cols = pl.ds(j * TILE, TILE)
            part[rows, cols] = jnp.dot(om, wod[:, cols], preferred_element_type=F32).astype(BF16)

    def chip_sum(t):
        copy(SWAP, t).wait_recv()
        for i in range(4):
            n = half // 4
            rows = pl.ds(pl.multiple_of(t * ROWS + core * half + i * n, n), n)
            got = swap[pl.ds(pl.multiple_of(t * half + i * n, n), n), :].astype(F32)
            part[rows, :] = (part[rows, :].astype(F32) + got).astype(BF16)
        for kind in (FWD_R, FWD_L, OWN_R, OWN_L):
            copy(kind, t).start()

    def pass_on(t):
        for kind, out, c, cols in ((FWD_R, SUM_R, c_r, A), (FWD_L, SUM_L, c_l, B)):
            copy(kind, t).wait_recv()
            rows = rows_of(t, c)
            part[rows, cols] = (part[rows, cols].astype(F32) + fwd[slot(t), cols].astype(F32)).astype(BF16)
            copy(out, t).start()

    def finish(t):
        for kind in (OWN_R, OWN_L, SUM_R, SUM_L):
            copy(kind, t).wait_recv()
        rows = rows_of(t, chip)
        total = (part[rows, :].astype(F32) + from_l[slot(t), :].astype(F32)) + from_r[slot(t), :].astype(F32)
        y_ref[rows, :] = (x_v[rows, :].astype(F32) + total).astype(BF16)
        for kind in (OUT_R, OUT_L, OUT_P):
            copy(kind, t).start()

    def spread(t):
        copy(OUT_R, t).wait_recv()
        copy(FAR_R, t).start()
        copy(P_LEFT, t).start()
        copy(OUT_L, t).wait_recv()
        copy(FAR_L, t).start()
        copy(P_RIGHT, t).start()

    def far(t):
        copy(FAR_R, t).wait_recv()
        copy(P_FAR_A, t).start()
        copy(FAR_L, t).wait_recv()
        copy(P_FAR_B, t).start()

    def close(t):
        for kind in (OUT_P, P_LEFT, P_RIGHT, P_FAR_A, P_FAR_B):
            copy(kind, t).wait_recv()
        for kind in range(N_KINDS):
            copy(kind, t).wait_send()

    def at(t, fn):
        @pl.when(jnp.logical_and(t >= 0, t < blocks))
        def _():
            fn(t)

    def step(s, _):
        @pl.when(s < blocks)
        def _():
            project(s)
            attend(s)
            mlp(s)

            @pl.when(s == 0)
            def _():
                for cp in w_loads[5:]:
                    cp.wait()
            out_half(s, 1 - core)
            copy(SWAP, s).start()
            out_half(s, core)
            chip_sum(s)
        at(s - 1, pass_on)
        at(s - 2, finish)
        at(s - 3, spread)
        at(s - 4, far)
        at(s - 5, close)
        return 0

    lax.fori_loop(0, blocks + 5, step, 0)


def solution(mesh):
    n_tp = mesh.shape['tp']

    def local_layer(x_in, g_norm, w_q, w_k, w_v, w_o, w_gate, w_up, w_down):
        tokens, width = x_in.shape
        blocks = tokens // ROWS
        qw, ff = w_q.shape[1], w_gate.shape[1]
        heads = qw // HEAD_DIM
        half = ROWS // 2
        chunk = half // (n_tp // 2)
        consts = [jnp.asarray(c) for c in rope_constants(ROWS, blocks)]
        vm = lambda: pl.BlockSpec(memory_space=pltpu.VMEM)
        hbm = lambda: pl.BlockSpec(memory_space=pl.ANY)
        y_out, k_rot, v_proj = pl.pallas_call(
            functools.partial(layer_kernel, n_tp),
            out_shape=(jax.ShapeDtypeStruct((tokens, width), BF16),
                       jax.ShapeDtypeStruct((tokens, HEAD_DIM), BF16),
                       jax.ShapeDtypeStruct((tokens, HEAD_DIM), BF16)),
            in_specs=[hbm(), vm()] + [hbm()] * 7 + [vm()] * 4,
            out_specs=(vm(), vm(), vm()),
            scratch_shapes=[
                pltpu.VMEM((tokens, width), BF16),
                pltpu.VMEM((width, qw + 2 * HEAD_DIM), BF16),
                pltpu.VMEM((width, 2 * ff), BF16),
                pltpu.VMEM((qw + ff, width), BF16),
                pltpu.VMEM((ROWS, width), BF16),
                pltpu.VMEM((heads * ROWS, HEAD_DIM), BF16),
                pltpu.VMEM((tokens // KEYS, heads * ROWS, KEYS), F32),
                pltpu.VMEM((heads * ROWS, 128), F32),
                pltpu.VMEM((heads * ROWS, 128), F32),
                pltpu.VMEM((heads * ROWS, HEAD_DIM), F32),
                pltpu.VMEM((ROWS, qw + ff), BF16),
                pltpu.VMEM((tokens, width), BF16),
                pltpu.VMEM((tokens // 2, width), BF16),
                pltpu.VMEM((blocks * chunk, width), BF16),
                pltpu.VMEM((blocks * chunk, width), BF16),
                pltpu.VMEM((blocks * chunk, width), BF16),
                pltpu.SemaphoreType.DMA((8 + blocks,)),
                pltpu.SemaphoreType.DMA((N_KINDS, blocks)),
                pltpu.SemaphoreType.DMA((N_KINDS, blocks)),
            ],
            compiler_params=pltpu.CompilerParams(
                collective_id=0, has_side_effects=True, vmem_limit_bytes=67043328),
            name='layer',
        )(x_in, g_norm.reshape(1, width), w_q, w_k, w_v, w_o, w_gate, w_up, w_down, *consts)
        return y_out, k_rot.reshape(tokens, 1, HEAD_DIM), v_proj.reshape(tokens, 1, HEAD_DIM)

    return jax.shard_map(local_layer, mesh=mesh, in_specs=(P('dp', None), P(None), P(None, 'tp'), P(None, None), P(None, None), P('tp', None), P(None, 'tp'), P(None, 'tp'), P('tp', None)), out_specs=(P('dp', None), P('dp', 'tp', None), P('dp', 'tp', None)), check_vma=False)
```

time: 309 us -> 94.2 us (0.30)
  matrix products: 147 us -> 0 us
  Pallas kernels: 0 us -> 83.9 us
  waiting for transfers between devices: 78.8 us -> 0 us
  other arithmetic: 33.2 us -> 0 us
  local copies, waits for them, and re-layouts: 23.7 us -> 9.48 us
  between operations: 14.2 us -> 0.66 us
  loops' own time: 9.18 us -> 0 us
    dot_general x74 -> x0, matrix products: 147 us -> none  [the longest x12 60.9 us: row_block(): jnp.dot(hidden, w_down, preferred_element_type=jnp.float32)]
    pallas_call x0 -> x1, Pallas kernels: none -> 83.9 us  [local_layer(): pl.pallas_call(functools.partial(layer_kernel, n_tp), out_shape=(jax.Shap...]
    psum x1 -> x0, waiting for transfers between devices: 78.7 us -> none  [local_layer(): reduced_sum = lax.psum(partial_sum, 'tp')]
    dynamic_slice x24 -> x0, local copies, waits for them, and re-layouts: 18.5 us -> none  [the longest x12 10.6 us: row_block(): sin_blk = lax.dynamic_slice_in_dim(sin_tab, row_start, q_block, axis=0)]
    convert_element_type x4 -> x0, other arithmetic: 15.3 us -> none  [the longest x1 11 us: local_layer(): (x_in.astype(jnp.float32) + reduced_sum.astype(jnp.float32)).astype(jnp.b...]
    another operation x1 -> x0, loops' own time: 9.18 us -> none  [local_layer(): lax.map(row_block, jnp.arange(tokens // q_block)).reshape(tokens, width)]
    reduce_sum x13 -> x0, other arithmetic: 8.48 us -> none  [the longest x12 4.4 us: row_block(): probs_bf = jax.nn.softmax(scores, axis=-1).astype(jnp.bfloat16)]
    unnamed x12 -> x7, local copies, waits for them, and re-layouts: 1.89 us -> 8.18 us
  transfers between devices with their start and end apart: 1 -> 0, of which waited for: 1 -> 0; matrix products, arithmetic and copies ran while one was open for 0% -> 0% of each run, Pallas kernels for 0% -> 0%
where the time goes in v1:
time: 94.2 us; the launch traced here: 94.1 us
  Pallas kernels  83.9 us (89%)
  local copies, waits for them, and re-layouts  9.48 us (10%)
    pallas_call x1, Pallas kernels, local_layer(): pl.pallas_call(functools.partial(layer_kernel, n_tp), out_shape=(jax.Shap...  83.9 us
    unnamed x7, local copies, waits for them, and re-layouts  8.18 us

profile of v1, /device:TPU:113, one launch (start us, length us, event | category | flops | bytes accessed | tf_op | source)
XLA Modules:
  0.0 94.1 jit_solution(16350375566817858371)
XLA Ops:
  0.6 1.3 %reshape.15.g_ref = bf16[1,2048]{1,0:T(2,128)(2,1)} reshape(bf16[2048]{0:T(1024)(128)(2,1)} %param.14) | data formatting | bytes 8192 | tf_op jit(solution)/shard_map/reshape | solution.py:335
  1.9 83.9 %layer.1 = (bf16[1536,2048]{1,0:T(8,128)(2,1)}, bf16[1536,128]{1,0:T(8,128)(2,1)}, bf16[1536,128]{1,0:T(8,128)(2,1)}) custom-call(bf16[1536,2048]{1,0:T(8,128)(2,1)} %x_hbm.1, bf16[1,2048]{1,0:T(2,128)(2,1)} %reshape.15.g_ref, bf16[2048,256]{1,0:T(8,128)(2,1)} %wq_hbm.1, bf16[2048,1024]{1,0:T(8,128)(2,1)} %wk_hbm.1, bf16[2048,1024]{1,0:T(8,128)(2,1)} %wv_hbm.1, ...), custom_call_target="tpu_custom_call" | custom-call | tf_op jit(solution)/shard_map/layer/pallas_call | solution.py:304
  85.9 0.0 copy-start.1
  85.9 0.0 copy-start
  85.9 6.7 %copy.19 = bf16[1536,2048]{1,0:T(8,128)(2,1)} copy(bf16[1536,2048]{1,0:T(8,128)(2,1)} %get-tuple-element.12) | data formatting | bytes 12582912
  92.6 0.0 copy-done.1
  92.6 0.7 copy.20
  93.3 0.0 copy-done
  93.3 0.7 copy.21
Async XLA Ops:
  85.9 6.7 %copy-start.1 = (bf16[1536,128]{1,0:T(8,128)(2,1)S(1)}, bf16[1536,128]{1,0:T(8,128)(2,1)}, u32[]{:S(2)}) copy-start(bf16[1536,128]{1,0:T(8,128)(2,1)} %get-tuple-element.7) | copy-start | bytes 1179652
  85.9 7.4 %copy-start = (bf16[1536,128]{1,0:T(8,128)(2,1)S(1)}, bf16[1536,128]{1,0:T(8,128)(2,1)}, u32[]{:S(2)}) copy-start(bf16[1536,128]{1,0:T(8,128)(2,1)} %get-tuple-element.8) | copy-start | bytes 1179652

commit v2 on v1

v2 whole, which is shorter than its diff:
```python
import functools
import math
import numpy as np
import jax
import jax.numpy as jnp
from jax import lax
from jax.experimental import pallas as pl
from jax.experimental.pallas import tpu as pltpu
from jax.sharding import PartitionSpec as P

HEAD_DIM = 128
ROPE_BASE = 500000.0
NORM_EPS = 1e-5
ROWS = 256
TILE = 256
STORES = 8
F32 = jnp.float32
BF16 = jnp.bfloat16
MESH = pl.DeviceIdType.MESH

(SWAP_A, SWAP_B, FWD_R, OWN_L, FWD_L, OWN_R, SUM_R, SUM_L, OUT_R, OUT_L, OUT_P, FAR_R, FAR_L,
 P_LEFT, P_RIGHT, P_FAR_A, P_FAR_B) = range(17)
N_KINDS = 17

PLACES = {'start': (('pass_on_b', 2),),
          'project': (('chip_sum_a', 1), ('spread', 4), ('close', 7),),
          'values': (('chip_sum_b', 1),),
          'mlp1': (('finish', 2),),
          'out1': (('pass_on_a', 1), ('far', 4),)}
DRAIN = (('spread', 3), ('close', 5), ('chip_sum_a', 0), ('chip_sum_b', 0),
         ('pass_on_b', 1), ('close', 4), ('spread', 2), ('far', 3),
         ('pass_on_a', 0), ('close', 3), ('pass_on_b', 0), ('finish', 1),
         ('far', 2), ('close', 2), ('finish', 0), ('spread', 1),
         ('spread', 0), ('far', 1), ('close', 1), ('far', 0),
         ('close', 0),)


def rope_constants(rows, blocks):
    inv_freq = ROPE_BASE ** (-np.arange(0, HEAD_DIM, 2, dtype=np.float64) / HEAD_DIM)
    def tables(positions):
        ang = positions[:, None] * inv_freq[None, :]
        cos, sin = np.cos(ang), np.sin(ang)
        return (np.concatenate([cos, cos], 1).astype(np.float32),
                np.concatenate([-sin, sin], 1).astype(np.float32))
    cos_r, sin_r = tables(np.arange(rows, dtype=np.float64))
    cos_t, sin_t = tables(np.arange(blocks, dtype=np.float64) * rows)
    return cos_r, sin_r, cos_t, sin_t


def layer_kernel(n_tp, x_hbm, g_hbm, wq_hbm, wk_hbm, wv_hbm, wo_hbm, wg_hbm, wu_hbm, wd_hbm,
                 rope_r_hbm, rope_t_hbm, y_ref, k_ref, v_ref,
                 x_v, g_v, rope_r, rope_t, wqkv, wgu, wod, a_s, q_s, s_s, m_s, l_s, o_s, om_s,
                 part, swap, fwd, from_l, from_r, load_sem, send_sem, recv_sem):
    tokens, width = x_v.shape
    blocks = tokens // ROWS
    half = ROWS // 2
    n_chip = n_tp // 2
    chunk = half // n_chip
    wh = width // 2
    qw = wq_hbm.shape[1]
    heads = qw // HEAD_DIM
    ff = wg_hbm.shape[1]
    me = lax.axis_index('tp')
    chip, core = me // 2, lax.rem(me, 2)
    partner = chip * 2 + 1 - core
    c_r = lax.rem(chip + 1, n_chip)
    c_l = lax.rem(chip + n_chip - 1, n_chip)
    c_o = lax.rem(chip + 2, n_chip)
    right = c_r * 2 + core
    left = c_l * 2 + core

    kv_col = pl.multiple_of(me * HEAD_DIM, HEAD_DIM)
    def x_load(t):
        rows = pl.ds(pl.multiple_of(t * ROWS, ROWS), ROWS)
        return pltpu.make_async_copy(x_hbm.at[rows], x_v.at[rows], load_sem.at[8 + 2 * (ff // TILE) + t])
    def load(i, src, dst):
        return pltpu.make_async_copy(src, dst, load_sem.at[i])
    small_loads = [
        load(0, g_hbm, g_v),
        load(1, rope_r_hbm, rope_r),
        load(2, rope_t_hbm, rope_t),
    ]
    qkv_loads = [
        load(3, wq_hbm, wqkv.at[:, pl.ds(0, qw)]),
        load(4, wk_hbm.at[:, pl.ds(kv_col, HEAD_DIM)], wqkv.at[:, pl.ds(qw, HEAD_DIM)]),
        load(5, wv_hbm.at[:, pl.ds(kv_col, HEAD_DIM)], wqkv.at[:, pl.ds(qw + HEAD_DIM, HEAD_DIM)]),
    ]
    ff_tiles = ff // TILE
    mlp_loads = []
    for j in range(ff_tiles):
        cols, up_cols = pl.ds(j * TILE, TILE), pl.ds(ff + j * TILE, TILE)
        mlp_loads.append([load(8 + 2 * j, wg_hbm.at[:, cols], wgu.at[:, cols]),
                          load(9 + 2 * j, wu_hbm.at[:, cols], wgu.at[:, up_cols])])
    out_loads = [
        load(6, wo_hbm, wod.at[pl.ds(0, qw)]),
        load(7, wd_hbm, wod.at[pl.ds(qw, ff)]),
    ]
    x_load(0).start()
    for cp in small_loads + qkv_loads + sum(mlp_loads, []) + out_loads:
        cp.start()
    for t in range(1, blocks):
        x_load(t).start()

    def first(t, copies):
        @pl.when(t == 0)
        def _():
            for cp in copies:
                cp.wait()

    barrier = pltpu.get_barrier_semaphore()
    for dev in (partner, left, right):
        pl.semaphore_signal(barrier, inc=1, device_id={'tp': dev}, device_id_type=MESH)
    pl.semaphore_wait(barrier, 3)

    def rows_of(t, c):
        return pl.ds(pl.multiple_of(t * ROWS + core * half + c * chunk, chunk), chunk)

    def slot(t):
        return pl.ds(pl.multiple_of(t * chunk, chunk), chunk)

    A, B = pl.ds(0, wh), pl.ds(wh, wh)

    def copy(kind, t):
        other = pl.ds(pl.multiple_of(t * ROWS + (1 - core) * half, half), half)
        src, dst, dev = {
            SWAP_A: lambda: (part.at[other, A], swap.at[pl.ds(pl.multiple_of(t * half, half), half), A], partner),
            SWAP_B: lambda: (part.at[other, B], swap.at[pl.ds(pl.multiple_of(t * half, half), half), B], partner),
            FWD_R: lambda: (part.at[rows_of(t, c_o), A], fwd.at[slot(t), A], right),
            OWN_R: lambda: (part.at[rows_of(t, c_r), B], from_l.at[slot(t), B], right),
            FWD_L: lambda: (part.at[rows_of(t, c_o), B], fwd.at[slot(t), B], left),
            OWN_L: lambda: (part.at[rows_of(t, c_l), A], from_r.at[slot(t), A], left),
            SUM_R: lambda: (part.at[rows_of(t, c_r), A], from_l.at[slot(t), A], right),
            SUM_L: lambda: (part.at[rows_of(t, c_l), B], from_r.at[slot(t), B], left),
            OUT_R: lambda: (y_ref.at[rows_of(t, chip)], y_ref.at[rows_of(t, chip)], right),
            OUT_L: lambda: (y_ref.at[rows_of(t, chip)], y_ref.at[rows_of(t, chip)], left),
            OUT_P: lambda: (y_ref.at[rows_of(t, chip)], y_ref.at[rows_of(t, chip)], partner),
            FAR_R: lambda: (y_ref.at[rows_of(t, c_l), A], y_ref.at[rows_of(t, c_l), A], right),
            FAR_L: lambda: (y_ref.at[rows_of(t, c_r), B], y_ref.at[rows_of(t, c_r), B], left),
            P_LEFT: lambda: (y_ref.at[rows_of(t, c_l)], y_ref.at[rows_of(t, c_l)], partner),
            P_RIGHT: lambda: (y_ref.at[rows_of(t, c_r)], y_ref.at[rows_of(t, c_r)], partner),
            P_FAR_A: lambda: (y_ref.at[rows_of(t, c_o), A], y_ref.at[rows_of(t, c_o), A], partner),
            P_FAR_B: lambda: (y_ref.at[rows_of(t, c_o), B], y_ref.at[rows_of(t, c_o), B], partner),
        }[kind]()
        return pltpu.make_async_remote_copy(
            src_ref=src, dst_ref=dst, send_sem=send_sem.at[kind, t], recv_sem=recv_sem.at[kind, t],
            device_id={'tp': dev}, device_id_type=MESH)

    scale = 1.0 / math.sqrt(HEAD_DIM) * math.log2(math.e)

    def project(t):
        x_load(t).wait()
        first(t, small_loads)
        step = 64
        gain = g_v[...].astype(F32).reshape(1, width)
        for i in range(ROWS // step):
            xf = x_v[pl.ds(pl.multiple_of(t * ROWS + i * step, step), step), :].astype(F32)
            inv = lax.rsqrt(jnp.mean(xf * xf, axis=-1, keepdims=True) + NORM_EPS)
            a_s[pl.ds(i * step, step), :] = (xf * inv * gain).astype(BF16)
        first(t, qkv_loads)
        a = a_s[...]
        c0, s0 = rope_t[0, pl.ds(t, 1), :], rope_t[1, pl.ds(t, 1), :]
        cos = rope_r[0] * c0 - rope_r[1] * s0
        sin = rope_r[1] * c0 + rope_r[0] * s0
        rot = lambda p: (p * cos + pltpu.roll(p, HEAD_DIM // 2, 1) * sin).astype(BF16)
        q = jnp.dot(a, wqkv[:, pl.ds(0, qw)], preferred_element_type=F32)
        kv = jnp.dot(a, wqkv[:, pl.ds(qw, 2 * HEAD_DIM)], preferred_element_type=F32)
        for h in range(heads):
            q_s[pl.ds(h * ROWS, ROWS), :] = rot(q[:, h * HEAD_DIM:(h + 1) * HEAD_DIM])
        rows = pl.ds(pl.multiple_of(t * ROWS, ROWS), ROWS)
        k_ref[rows, :] = rot(kv[:, :HEAD_DIM])
        v_ref[rows, :] = kv[:, HEAD_DIM:].astype(BF16)

    def lanes(op, s):
        acc = s[:, :128]
        for i in range(1, ROWS // 128):
            acc = op(acc, s[:, i * 128:(i + 1) * 128])
        return acc

    def keys(kb):
        return pl.ds(pl.multiple_of(kb * ROWS, ROWS), ROWS)

    def score(kb):
        return lax.dot_general(q_s[...], k_ref[keys(kb), :], (((1,), (1,)), ((), ())), preferred_element_type=F32)

    def attend_scores(t):
        s = score(t)
        shape = (heads, ROWS, ROWS)
        q_pos = lax.broadcasted_iota(jnp.int32, shape, 1).reshape(heads * ROWS, ROWS)
        k_pos = lax.broadcasted_iota(jnp.int32, shape, 2).reshape(heads * ROWS, ROWS)
        s = jnp.where(k_pos <= q_pos, s, -1e30)
        s_s[t] = s
        m_s[...] = lanes(jnp.maximum, s)

        def pass1(kb, _):
            s = score(kb)
            s_s[kb] = s
            m_s[...] = jnp.maximum(m_s[...], lanes(jnp.maximum, s))
            return 0
        lax.fori_loop(0, t, pass1, 0)
        m_s[...] = jnp.broadcast_to(jnp.max(m_s[...], axis=-1, keepdims=True) * scale, m_s.shape)
        l_s[...] = jnp.zeros_like(l_s)

        def pass2(kb, _):
            m = m_s[...]
            p = jnp.exp2(s_s[kb] * scale - jnp.concatenate([m] * (ROWS // 128), axis=1))
            s_s[kb] = p
            l_s[...] += lanes(jnp.add, p)
            return 0
        lax.fori_loop(0, t + 1, pass2, 0)

    def attend_values(t):
        l_s[...] = jnp.broadcast_to(1.0 / jnp.sum(l_s[...], axis=-1, keepdims=True), l_s.shape)
        o_s[...] = jnp.zeros_like(o_s)

        def pass3(kb, _):
            r = l_s[...]
            p = (s_s[kb] * jnp.concatenate([r] * (ROWS // 128), axis=1)).astype(BF16)
            o_s[...] += jnp.dot(p, v_ref[keys(kb), :], preferred_element_type=F32)
            return 0
        lax.fori_loop(0, t + 1, pass3, 0)
        for h in range(heads):
            om_s[:, pl.ds(h * HEAD_DIM, HEAD_DIM)] = o_s[pl.ds(h * ROWS, ROWS), :].astype(BF16)

    def mlp(t, j):
        first(t, mlp_loads[j])
        a = a_s[...]
        gate = jnp.dot(a, wgu[:, pl.ds(j * TILE, TILE)], preferred_element_type=F32)
        up = jnp.dot(a, wgu[:, pl.ds(ff + j * TILE, TILE)], preferred_element_type=F32)
        om_s[:, pl.ds(qw + j * TILE, TILE)] = (jax.nn.silu(gate) * up).astype(BF16)

    def out_half(t, which, kind):
        om = om_s[...]
        rows = pl.ds(pl.multiple_of(t * ROWS, ROWS), ROWS)
        tiles = width // TILE // 2
        for j in range(which * tiles, (which + 1) * tiles):
            cols = pl.ds(j * TILE, TILE)
            part[rows, cols] = jnp.dot(om, wod[:, cols], preferred_element_type=F32).astype(BF16)
        copy(kind, t).start()

    def chip_sum(t, cols, got, *sends):
        copy(got, t).wait_recv()
        for i in range(4):
            n = half // 4
            rows = pl.ds(pl.multiple_of(t * ROWS + core * half + i * n, n), n)
            other = swap[pl.ds(pl.multiple_of(t * half + i * n, n), n), cols].astype(F32)
            part[rows, cols] = (part[rows, cols].astype(F32) + other).astype(BF16)
        for kind in sends:
            copy(kind, t).start()

    def pass_on(t, cols, got, out, c):
        copy(got, t).wait_recv()
        rows = rows_of(t, c)
        part[rows, cols] = (part[rows, cols].astype(F32) + fwd[slot(t), cols].astype(F32)).astype(BF16)
        copy(out, t).start()

    def finish(t):
        for kind in (OWN_R, OWN_L, SUM_R, SUM_L):
            copy(kind, t).wait_recv()
        rows = rows_of(t, chip)
        total = (part[rows, :].astype(F32) + from_l[slot(t), :].astype(F32)) + from_r[slot(t), :].astype(F32)
        y_ref[rows, :] = (x_v[rows, :].astype(F32) + total).astype(BF16)
        for kind in (OUT_R, OUT_L, OUT_P):
            copy(kind, t).start()

    def spread(t):
        copy(OUT_R, t).wait_recv()
        copy(FAR_R, t).start()
        copy(P_LEFT, t).start()
        copy(OUT_L, t).wait_recv()
        copy(FAR_L, t).start()
        copy(P_RIGHT, t).start()

    def far(t):
        copy(FAR_R, t).wait_recv()
        copy(P_FAR_A, t).start()
        copy(FAR_L, t).wait_recv()
        copy(P_FAR_B, t).start()

    def close(t):
        for kind in (OUT_P, P_LEFT, P_RIGHT, P_FAR_A, P_FAR_B):
            copy(kind, t).wait_recv()
        for kind in range(N_KINDS):
            copy(kind, t).wait_send()

    stages = {
        'chip_sum_a': lambda t: chip_sum(t, A, SWAP_A, FWD_R, OWN_L),
        'chip_sum_b': lambda t: chip_sum(t, B, SWAP_B, FWD_L, OWN_R),
        'pass_on_a': lambda t: pass_on(t, A, FWD_R, SUM_R, c_r),
        'pass_on_b': lambda t: pass_on(t, B, FWD_L, SUM_L, c_l),
        'finish': finish, 'spread': spread, 'far': far, 'close': close,
    }

    def place(p, s):
        for name, lag in PLACES.get(p, ()):
            @pl.when(s >= lag)
            def _(name=name, lag=lag):
                stages[name](s - lag)

    def step(s, _):
        place('start', s)
        project(s)
        place('project', s)
        attend_scores(s)
        place('scores', s)
        attend_values(s)
        place('values', s)
        for j in range(ff_tiles):
            mlp(s, j)
            place('mlp%d' % j, s)
        first(s, out_loads)
        out_half(s, 0, SWAP_A)
        place('out0', s)
        out_half(s, 1, SWAP_B)
        place('out1', s)
        return 0

    lax.fori_loop(0, blocks, step, 0)
    for name, back in DRAIN:
        stages[name](blocks - 1 - back)


def store_kernel(y_ref, k_ref, v_ref, y_hbm, k_hbm, v_hbm, sem):
    n = y_ref.shape[0] // STORES
    copies = [pltpu.make_async_copy(y_ref.at[pl.ds(i * n, n)], y_hbm.at[pl.ds(i * n, n)], sem.at[2 + i])
              for i in range(STORES)]
    copies += [pltpu.make_async_copy(k_ref, k_hbm, sem.at[0]), pltpu.make_async_copy(v_ref, v_hbm, sem.at[1])]
    for cp in copies:
        cp.start()
    for cp in copies:
        cp.wait()


def solution(mesh):
    n_tp = mesh.shape['tp']

    def local_layer(x_in, g_norm, w_q, w_k, w_v, w_o, w_gate, w_up, w_down):
        tokens, width = x_in.shape
        blocks = tokens // ROWS
        qw, ff = w_q.shape[1], w_gate.shape[1]
        heads = qw // HEAD_DIM
        half = ROWS // 2
        chunk = half // (n_tp // 2)
        cos_r, sin_r, cos_t, sin_t = rope_constants(ROWS, blocks)
        consts = [jnp.asarray(np.stack([cos_r, sin_r])), jnp.asarray(np.stack([cos_t, sin_t]))]
        vm = lambda: pl.BlockSpec(memory_space=pltpu.VMEM)
        hbm = lambda: pl.BlockSpec(memory_space=pl.ANY)
        y_out, k_rot, v_proj = pl.pallas_call(
            functools.partial(layer_kernel, n_tp),
            out_shape=(pltpu.VMEM((tokens, width), BF16),
                       pltpu.VMEM((tokens, HEAD_DIM), BF16),
                       pltpu.VMEM((tokens, HEAD_DIM), BF16)),
            in_specs=[hbm()] * 11,
            out_specs=(vm(), vm(), vm()),
            scratch_shapes=[
                pltpu.VMEM((tokens, width), BF16),
                pltpu.VMEM((width,), BF16),
                pltpu.VMEM((2, ROWS, HEAD_DIM), F32),
                pltpu.VMEM((2, blocks, HEAD_DIM), F32),
                pltpu.VMEM((width, qw + 2 * HEAD_DIM), BF16),
                pltpu.VMEM((width, 2 * ff), BF16),
                pltpu.VMEM((qw + ff, width), BF16),
                pltpu.VMEM((ROWS, width), BF16),
                pltpu.VMEM((heads * ROWS, HEAD_DIM), BF16),
                pltpu.VMEM((tokens // ROWS, heads * ROWS, ROWS), F32),
                pltpu.VMEM((heads * ROWS, 128), F32),
                pltpu.VMEM((heads * ROWS, 128), F32),
                pltpu.VMEM((heads * ROWS, HEAD_DIM), F32),
                pltpu.VMEM((ROWS, qw + ff), BF16),
                pltpu.VMEM((tokens, width), BF16),
                pltpu.VMEM((tokens // 2, width), BF16),
                pltpu.VMEM((blocks * chunk, width), BF16),
                pltpu.VMEM((blocks * chunk, width), BF16),
                pltpu.VMEM((blocks * chunk, width), BF16),
                pltpu.SemaphoreType.DMA((8 + 2 * (ff // TILE) + blocks,)),
                pltpu.SemaphoreType.DMA((N_KINDS, blocks)),
                pltpu.SemaphoreType.DMA((N_KINDS, blocks)),
            ],
            compiler_params=pltpu.CompilerParams(
                collective_id=0, has_side_effects=True, vmem_limit_bytes=52 * 2**20),
            name='layer',
        )(x_in, g_norm, w_q, w_k, w_v, w_o, w_gate, w_up, w_down, *consts)
        y_out, k_rot, v_proj = pl.pallas_call(
            store_kernel,
            out_shape=tuple(jax.ShapeDtypeStruct(a.shape, BF16) for a in (y_out, k_rot, v_proj)),
            in_specs=[vm()] * 3, out_specs=(hbm(),) * 3,
            scratch_shapes=[pltpu.SemaphoreType.DMA((2 + STORES,))],
            compiler_params=pltpu.CompilerParams(vmem_limit_bytes=8 * 2**20),
            name='store',
        )(y_out, k_rot, v_proj)
        return y_out, k_rot.reshape(tokens, 1, HEAD_DIM), v_proj.reshape(tokens, 1, HEAD_DIM)

    return jax.shard_map(local_layer, mesh=mesh, in_specs=(P('dp', None), P(None), P(None, 'tp'), P(None, None), P(None, None), P('tp', None), P(None, 'tp'), P(None, 'tp'), P('tp', None)), out_specs=(P('dp', None), P('dp', 'tp', None), P('dp', 'tp', None)), check_vma=False)
```

time: 94.2 us -> 78.1 us (0.83)
  local copies, waits for them, and re-layouts: 9.48 us -> 0 us
  Pallas kernels: 83.9 us -> 77.4 us
    unnamed x7 -> x0, local copies, waits for them, and re-layouts: 8.18 us -> none
    pallas_call x1 -> x2, Pallas kernels: 83.9 us -> 77.4 us  [the longest x1 74.4 us: local_layer(): pl.pallas_call(functools.partial(layer_kernel, n_tp), out_shape=(pltpu.VM...]
    reshape x1 -> x0, local copies, waits for them, and re-layouts: 1.29 us -> none  [local_layer(): g_norm.reshape(1, width)]
where the time goes in v2:
time: 78.1 us
  Pallas kernels  77.4 us (99%)
    pallas_call x1, Pallas kernels, local_layer(): pl.pallas_call(functools.partial(layer_kernel, n_tp), out_shape=(pltpu.VM...  74.4 us
    pallas_call x1, Pallas kernels, local_layer(): pl.pallas_call(store_kernel, out_shape=tuple((jax.ShapeDtypeStruct(a.shap...  2.98 us

profile of v2, /device:TPU:113, one launch (start us, length us, event | category | flops | bytes accessed | tf_op | source)
XLA Modules:
  0.0 78.1 jit_solution(3039065203946785620)
XLA Ops:
  0.6 74.4 %layer.1 = (bf16[1536,2048]{1,0:T(8,128)(2,1)S(1)}, bf16[1536,128]{1,0:T(8,128)(2,1)S(1)}, bf16[1536,128]{1,0:T(8,128)(2,1)S(1)}) custom-call(bf16[1536,2048]{1,0:T(8,128)(2,1)} %x_hbm.1, bf16[2048]{0:T(1024)(128)(2,1)} %g_hbm.1, bf16[2048,256]{1,0:T(8,128)(2,1)} %wq_hbm.1, bf16[2048,1024]{1,0:T(8,128)(2,1)} %wk_hbm.1, bf16[2048,1024]{1,0:T(8,128)(2,1)} %wv_hbm.1, ...), custom_call_target="tpu_custom_call" | custom-call | tf_op jit(solution)/shard_map/layer/pallas_call | solution.py:347
  75.1 3.0 %store.1 = (bf16[1536,2048]{1,0:T(8,128)(2,1)}, bf16[1536,128]{1,0:T(8,128)(2,1)}, bf16[1536,128]{1,0:T(8,128)(2,1)}) custom-call(bf16[1536,2048]{1,0:T(8,128)(2,1)S(1)} %get-tuple-element.9.y_ref, bf16[1536,128]{1,0:T(8,128)(2,1)S(1)} %get-tuple-element.10.k_ref, bf16[1536,128]{1,0:T(8,128)(2,1)S(1)} %get-tuple-element.11.v_ref), custom_call_target="tpu_custom_call" | custom-call | tf_op jit(solution)/shard_map/store/pallas_call | solution.py:382

commit v3 on v2

--- a/solution.py
+++ b/solution.py
@@ -20,19 +20,43 @@
 
 (SWAP_A, SWAP_B, FWD_R, OWN_L, FWD_L, OWN_R, SUM_R, SUM_L, OUT_R, OUT_L, OUT_P, FAR_R, FAR_L,
  P_LEFT, P_RIGHT, P_FAR_A, P_FAR_B) = range(17)
-N_KINDS = 17
-
-PLACES = {'start': (('pass_on_b', 2),),
-          'project': (('chip_sum_a', 1), ('spread', 4), ('close', 7),),
-          'values': (('chip_sum_b', 1),),
-          'mlp1': (('finish', 2),),
-          'out1': (('pass_on_a', 1), ('far', 4),)}
-DRAIN = (('spread', 3), ('close', 5), ('chip_sum_a', 0), ('chip_sum_b', 0),
-         ('pass_on_b', 1), ('close', 4), ('spread', 2), ('far', 3),
-         ('pass_on_a', 0), ('close', 3), ('pass_on_b', 0), ('finish', 1),
-         ('far', 2), ('close', 2), ('finish', 0), ('spread', 1),
-         ('spread', 0), ('far', 1), ('close', 1), ('far', 0),
-         ('close', 0),)
+R_SWAP_A, R_SWAP_B, R_FWD_R, R_FWD_L, R_FIN, R_OUT, R_FAR = range(7)
+N_RECV = 7
+ARRIVES = {SWAP_A: R_SWAP_A, SWAP_B: R_SWAP_B, FWD_R: R_FWD_R, FWD_L: R_FWD_L, OWN_L: R_FIN, OWN_R: R_FIN,
+           SUM_R: R_FIN, SUM_L: R_FIN, OUT_R: R_OUT, OUT_L: R_OUT, FAR_R: R_FAR, FAR_L: R_FAR}
+S_SWAP, S_LINK, S_PARTNER = range(3)
+
+PLACES = {
+    (1, 'project'): (('chip_sum_a', 0),),
+    (1, 'values'): (('chip_sum_b', 0),),
+    (1, 'out1'): (('pass_on_a', 0),),
+    (2, 'start'): (('pass_on_b', 0),),
+    (2, 'project'): (('chip_sum_a', 1),),
+    (2, 'values'): (('chip_sum_b', 1),),
+    (2, 'mlp1'): (('finish', 0),),
+    (2, 'out1'): (('pass_on_a', 1),),
+    (3, 'start'): (('pass_on_b', 1),),
+    (3, 'project'): (('chip_sum_a', 2),),
+    (3, 'values'): (('chip_sum_b', 2),),
+    (3, 'mlp1'): (('finish', 1),),
+    (3, 'out1'): (('pass_on_a', 2),),
+    (4, 'start'): (('pass_on_b', 2),),
+    (4, 'project'): (('spread', 0), ('chip_sum_a', 3),),
+    (4, 'values'): (('chip_sum_b', 3),),
+    (4, 'mlp1'): (('finish', 2),),
+    (4, 'out1'): (('far', 0), ('pass_on_a', 3),),
+    (5, 'start'): (('pass_on_b', 3),),
+    (5, 'project'): (('spread', 1), ('chip_sum_a', 4),),
+    (5, 'values'): (('chip_sum_b', 4),),
+    (5, 'mlp1'): (('finish', 3),),
+    (5, 'out1'): (('far', 1), ('pass_on_a', 4),),
+}
+DRAIN = (
+    ('spread', 2), ('chip_sum_a', 5), ('chip_sum_b', 5), ('pass_on_b', 4),
+    ('spread', 3), ('far', 2), ('pass_on_a', 5), ('pass_on_b', 5),
+    ('finish', 4), ('far', 3), ('finish', 5), ('spread', 4),
+    ('spread', 5), ('far', 4), ('far', 5),
+)
 
 
 def rope_constants(rows, blocks):
@@ -48,9 +72,9 @@
 
 
 def layer_kernel(n_tp, x_hbm, g_hbm, wq_hbm, wk_hbm, wv_hbm, wo_hbm, wg_hbm, wu_hbm, wd_hbm,
-                 rope_r_hbm, rope_t_hbm, y_ref, k_ref, v_ref,
-                 x_v, g_v, rope_r, rope_t, wqkv, wgu, wod, a_s, q_s, s_s, m_s, l_s, o_s, om_s,
-                 part, swap, fwd, from_l, from_r, load_sem, send_sem, recv_sem):
+                 rope_hbm, y_ref, k_ref, v_ref,
+                 x_v, g_v, rope, wqkv, wgu, wod, a_s, q_s, s_s, m_s, l_s, o_s, om_s,
+                 part, swap, fwd, from_l, from_r, load_sem, send_sem, recv_sem, done_sem):
     tokens, width = x_v.shape
     blocks = tokens // ROWS
     half = ROWS // 2
@@ -69,56 +93,49 @@
     right = c_r * 2 + core
     left = c_l * 2 + core
 
+    A, B = pl.ds(0, wh), pl.ds(wh, wh)
+
     kv_col = pl.multiple_of(me * HEAD_DIM, HEAD_DIM)
     def x_load(t):
         rows = pl.ds(pl.multiple_of(t * ROWS, ROWS), ROWS)
-        return pltpu.make_async_copy(x_hbm.at[rows], x_v.at[rows], load_sem.at[8 + 2 * (ff // TILE) + t])
+        return pltpu.make_async_copy(x_hbm.at[rows], x_v.at[rows], load_sem.at[5 + ff // TILE + t])
     def load(i, src, dst):
         return pltpu.make_async_copy(src, dst, load_sem.at[i])
-    small_loads = [
-        load(0, g_hbm, g_v),
-        load(1, rope_r_hbm, rope_r),
-        load(2, rope_t_hbm, rope_t),
+    ff_tiles = ff // TILE
+    L_SMALL, L_QKV, L_OUT, L_MLP, L_X = 0, 2, 3, 5, 5 + ff_tiles
+    small_loads = [load(L_SMALL, g_hbm, g_v), load(L_SMALL + 1, rope_hbm, rope)]
+    qkv_loads = [
+        load(L_QKV, wq_hbm, wqkv.at[:, pl.ds(0, qw)]),
+        load(L_QKV, wk_hbm.at[:, pl.ds(kv_col, HEAD_DIM)], wqkv.at[:, pl.ds(qw, HEAD_DIM)]),
+        load(L_QKV, wv_hbm.at[:, pl.ds(kv_col, HEAD_DIM)], wqkv.at[:, pl.ds(qw + HEAD_DIM, HEAD_DIM)]),
     ]
-    qkv_loads = [
-        load(3, wq_hbm, wqkv.at[:, pl.ds(0, qw)]),
-        load(4, wk_hbm.at[:, pl.ds(kv_col, HEAD_DIM)], wqkv.at[:, pl.ds(qw, HEAD_DIM)]),
-        load(5, wv_hbm.at[:, pl.ds(kv_col, HEAD_DIM)], wqkv.at[:, pl.ds(qw + HEAD_DIM, HEAD_DIM)]),
-    ]
-    ff_tiles = ff // TILE
     mlp_loads = []
     for j in range(ff_tiles):
         cols, up_cols = pl.ds(j * TILE, TILE), pl.ds(ff + j * TILE, TILE)
-        mlp_loads.append([load(8 + 2 * j, wg_hbm.at[:, cols], wgu.at[:, cols]),
-                          load(9 + 2 * j, wu_hbm.at[:, cols], wgu.at[:, up_cols])])
-    out_loads = [
-        load(6, wo_hbm, wod.at[pl.ds(0, qw)]),
-        load(7, wd_hbm, wod.at[pl.ds(qw, ff)]),
-    ]
+        mlp_loads += [load(L_MLP + j, wg_hbm.at[:, cols], wgu.at[:, cols]),
+                      load(L_MLP + j, wu_hbm.at[:, cols], wgu.at[:, up_cols])]
+    out_loads = []
+    for i, cols in enumerate((A, B)):
+        out_loads += [load(L_OUT + i, wo_hbm.at[:, cols], wod.at[pl.ds(0, qw), cols]),
+                      load(L_OUT + i, wd_hbm.at[:, cols], wod.at[pl.ds(qw, ff), cols])]
     x_load(0).start()
-    for cp in small_loads + qkv_loads + sum(mlp_loads, []) + out_loads:
+    for cp in small_loads + qkv_loads + mlp_loads + out_loads:
         cp.start()
     for t in range(1, blocks):
         x_load(t).start()
 
-    def first(t, copies):
-        @pl.when(t == 0)
-        def _():
-            for cp in copies:
-                cp.wait()
+    def loaded(t, sem, ref):
+        if t == 0:
+            load(sem, ref, ref).wait()
 
     barrier = pltpu.get_barrier_semaphore()
     for dev in (partner, left, right):
         pl.semaphore_signal(barrier, inc=1, device_id={'tp': dev}, device_id_type=MESH)
-    pl.semaphore_wait(barrier, 3)
-
     def rows_of(t, c):
         return pl.ds(pl.multiple_of(t * ROWS + core * half + c * chunk, chunk), chunk)
 
     def slot(t):
         return pl.ds(pl.multiple_of(t * chunk, chunk), chunk)
-
-    A, B = pl.ds(0, wh), pl.ds(wh, wh)
 
     def copy(kind, t):
         other = pl.ds(pl.multiple_of(t * ROWS + (1 - core) * half, half), half)
@@ -141,26 +158,35 @@
             P_FAR_A: lambda: (y_ref.at[rows_of(t, c_o), A], y_ref.at[rows_of(t, c_o), A], partner),
             P_FAR_B: lambda: (y_ref.at[rows_of(t, c_o), B], y_ref.at[rows_of(t, c_o), B], partner),
         }[kind]()
+        leaves = S_SWAP if kind in (SWAP_A, SWAP_B) else S_LINK if kind in ARRIVES else S_PARTNER
         return pltpu.make_async_remote_copy(
-            src_ref=src, dst_ref=dst, send_sem=send_sem.at[kind, t], recv_sem=recv_sem.at[kind, t],
+            src_ref=src, dst_ref=dst, send_sem=send_sem.at[leaves],
+            recv_sem=recv_sem.at[ARRIVES[kind], t] if kind in ARRIVES else done_sem.at[0],
             device_id={'tp': dev}, device_id_type=MESH)
+
+    def take(sem, rows):
+        ref = y_ref.at[pl.ds(0, rows)]
+        pltpu.make_async_copy(ref, ref, sem).wait()
 
     scale = 1.0 / math.sqrt(HEAD_DIM) * math.log2(math.e)
 
     def project(t):
         x_load(t).wait()
-        first(t, small_loads)
+        if t == 0:
+            for cp in small_loads:
+                cp.wait()
         step = 64
         gain = g_v[...].astype(F32).reshape(1, width)
         for i in range(ROWS // step):
             xf = x_v[pl.ds(pl.multiple_of(t * ROWS + i * step, step), step), :].astype(F32)
             inv = lax.rsqrt(jnp.mean(xf * xf, axis=-1, keepdims=True) + NORM_EPS)
             a_s[pl.ds(i * step, step), :] = (xf * inv * gain).astype(BF16)
-        first(t, qkv_loads)
+        loaded(t, L_QKV, wqkv)
         a = a_s[...]
-        c0, s0 = rope_t[0, pl.ds(t, 1), :], rope_t[1, pl.ds(t, 1), :]
-        cos = rope_r[0] * c0 - rope_r[1] * s0
-        sin = rope_r[1] * c0 + rope_r[0] * s0
+        c0, s0 = rope[0, pl.ds(ROWS + t, 1), :], rope[1, pl.ds(ROWS + t, 1), :]
+        cos_r, sin_r = rope[0, :ROWS, :], rope[1, :ROWS, :]
+        cos = cos_r * c0 - sin_r * s0
+        sin = sin_r * c0 + cos_r * s0
         rot = lambda p: (p * cos + pltpu.roll(p, HEAD_DIM // 2, 1) * sin).astype(BF16)
         q = jnp.dot(a, wqkv[:, pl.ds(0, qw)], preferred_element_type=F32)
         kv = jnp.dot(a, wqkv[:, pl.ds(qw, 2 * HEAD_DIM)], preferred_element_type=F32)
@@ -191,44 +217,39 @@
         s_s[t] = s
         m_s[...] = lanes(jnp.maximum, s)
 
-        def pass1(kb, _):
+        for kb in range(t):
             s = score(kb)
             s_s[kb] = s
             m_s[...] = jnp.maximum(m_s[...], lanes(jnp.maximum, s))
-            return 0
-        lax.fori_loop(0, t, pass1, 0)
         m_s[...] = jnp.broadcast_to(jnp.max(m_s[...], axis=-1, keepdims=True) * scale, m_s.shape)
         l_s[...] = jnp.zeros_like(l_s)
 
-        def pass2(kb, _):
+        for kb in range(t + 1):
             m = m_s[...]
             p = jnp.exp2(s_s[kb] * scale - jnp.concatenate([m] * (ROWS // 128), axis=1))
             s_s[kb] = p
             l_s[...] += lanes(jnp.add, p)
-            return 0
-        lax.fori_loop(0, t + 1, pass2, 0)
 
     def attend_values(t):
         l_s[...] = jnp.broadcast_to(1.0 / jnp.sum(l_s[...], axis=-1, keepdims=True), l_s.shape)
         o_s[...] = jnp.zeros_like(o_s)
 
-        def pass3(kb, _):
+        for kb in range(t + 1):
             r = l_s[...]
             p = (s_s[kb] * jnp.concatenate([r] * (ROWS // 128), axis=1)).astype(BF16)
             o_s[...] += jnp.dot(p, v_ref[keys(kb), :], preferred_element_type=F32)
-            return 0
-        lax.fori_loop(0, t + 1, pass3, 0)
         for h in range(heads):
             om_s[:, pl.ds(h * HEAD_DIM, HEAD_DIM)] = o_s[pl.ds(h * ROWS, ROWS), :].astype(BF16)
 
     def mlp(t, j):
-        first(t, mlp_loads[j])
+        loaded(t, L_MLP + j, wgu.at[:, pl.ds(0, 2 * TILE)])
         a = a_s[...]
         gate = jnp.dot(a, wgu[:, pl.ds(j * TILE, TILE)], preferred_element_type=F32)
         up = jnp.dot(a, wgu[:, pl.ds(ff + j * TILE, TILE)], preferred_element_type=F32)
         om_s[:, pl.ds(qw + j * TILE, TILE)] = (jax.nn.silu(gate) * up).astype(BF16)
 
     def out_half(t, which, kind):
+        loaded(t, L_OUT + which, wod.at[:, A])
         om = om_s[...]
         rows = pl.ds(pl.multiple_of(t * ROWS, ROWS), ROWS)
         tiles = width // TILE // 2
@@ -254,8 +275,7 @@
         copy(out, t).start()
 
     def finish(t):
-        for kind in (OWN_R, OWN_L, SUM_R, SUM_L):
-            copy(kind, t).wait_recv()
+        take(recv_sem.at[R_FIN, t], 2 * chunk)
         rows = rows_of(t, chip)
         total = (part[rows, :].astype(F32) + from_l[slot(t), :].astype(F32)) + from_r[slot(t), :].astype(F32)
         y_ref[rows, :] = (x_v[rows, :].astype(F32) + total).astype(BF16)
@@ -263,40 +283,28 @@
             copy(kind, t).start()
 
     def spread(t):
-        copy(OUT_R, t).wait_recv()
-        copy(FAR_R, t).start()
-        copy(P_LEFT, t).start()
-        copy(OUT_L, t).wait_recv()
-        copy(FAR_L, t).start()
-        copy(P_RIGHT, t).start()
+        take(recv_sem.at[R_OUT, t], 2 * chunk)
+        for kind in (FAR_R, FAR_L, P_LEFT, P_RIGHT):
+            copy(kind, t).start()
 
     def far(t):
-        copy(FAR_R, t).wait_recv()
-        copy(P_FAR_A, t).start()
-        copy(FAR_L, t).wait_recv()
-        copy(P_FAR_B, t).start()
-
-    def close(t):
-        for kind in (OUT_P, P_LEFT, P_RIGHT, P_FAR_A, P_FAR_B):
-            copy(kind, t).wait_recv()
-        for kind in range(N_KINDS):
-            copy(kind, t).wait_send()
+        take(recv_sem.at[R_FAR, t], chunk)
+        for kind in (P_FAR_A, P_FAR_B):
+            copy(kind, t).start()
 
     stages = {
         'chip_sum_a': lambda t: chip_sum(t, A, SWAP_A, FWD_R, OWN_L),
         'chip_sum_b': lambda t: chip_sum(t, B, SWAP_B, FWD_L, OWN_R),
         'pass_on_a': lambda t: pass_on(t, A, FWD_R, SUM_R, c_r),
         'pass_on_b': lambda t: pass_on(t, B, FWD_L, SUM_L, c_l),
-        'finish': finish, 'spread': spread, 'far': far, 'close': close,
+        'finish': finish, 'spread': spread, 'far': far,
     }
 
     def place(p, s):
-        for name, lag in PLACES.get(p, ()):
-            @pl.when(s >= lag)
-            def _(name=name, lag=lag):
-                stages[name](s - lag)
-
-    def step(s, _):
+        for name, t in PLACES.get((s, p), ()):
+            stages[name](t)
+
+    def step(s):
         place('start', s)
         project(s)
         place('project', s)
@@ -307,16 +315,21 @@
         for j in range(ff_tiles):
             mlp(s, j)
             place('mlp%d' % j, s)
-        first(s, out_loads)
+        if s == 0:
+            pl.semaphore_wait(barrier, 3)
         out_half(s, 0, SWAP_A)
         place('out0', s)
         out_half(s, 1, SWAP_B)
         place('out1', s)
-        return 0
-
-    lax.fori_loop(0, blocks, step, 0)
-    for name, back in DRAIN:
-        stages[name](blocks - 1 - back)
+
+    for s in range(blocks):
+        step(s)
+    for name, t in DRAIN:
+        stages[name](t)
+    take(done_sem.at[0], tokens // 2)
+    take(send_sem.at[S_SWAP], tokens // 2)
+    take(send_sem.at[S_LINK], tokens * 3 // 4)
+    take(send_sem.at[S_PARTNER], tokens // 2)
 
 
 def store_kernel(y_ref, k_ref, v_ref, y_hbm, k_hbm, v_hbm, sem):
@@ -341,7 +354,8 @@
         half = ROWS // 2
         chunk = half // (n_tp // 2)
         cos_r, sin_r, cos_t, sin_t = rope_constants(ROWS, blocks)
-        consts = [jnp.asarray(np.stack([cos_r, sin_r])), jnp.asarray(np.stack([cos_t, sin_t]))]
+        rope = np.stack([np.concatenate([cos_r, cos_t]), np.concatenate([sin_r, sin_t])])
+        rope = jnp.asarray(np.pad(rope, ((0, 0), (0, -blocks % 8), (0, 0))))
         vm = lambda: pl.BlockSpec(memory_space=pltpu.VMEM)
         hbm = lambda: pl.BlockSpec(memory_space=pl.ANY)
         y_out, k_rot, v_proj = pl.pallas_call(
@@ -349,13 +363,12 @@
             out_shape=(pltpu.VMEM((tokens, width), BF16),
                        pltpu.VMEM((tokens, HEAD_DIM), BF16),
                        pltpu.VMEM((tokens, HEAD_DIM), BF16)),
-            in_specs=[hbm()] * 11,
+            in_specs=[hbm()] * 10,
             out_specs=(vm(), vm(), vm()),
             scratch_shapes=[
                 pltpu.VMEM((tokens, width), BF16),
                 pltpu.VMEM((width,), BF16),
-                pltpu.VMEM((2, ROWS, HEAD_DIM), F32),
-                pltpu.VMEM((2, blocks, HEAD_DIM), F32),
+                pltpu.VMEM(rope.shape, F32),
                 pltpu.VMEM((width, qw + 2 * HEAD_DIM), BF16),
                 pltpu.VMEM((width, 2 * ff), BF16),
                 pltpu.VMEM((qw + ff, width), BF16),
@@ -371,14 +384,15 @@
                 pltpu.VMEM((blocks * chunk, width), BF16),
                 pltpu.VMEM((blocks * chunk, width), BF16),
                 pltpu.VMEM((blocks * chunk, width), BF16),
-                pltpu.SemaphoreType.DMA((8 + 2 * (ff // TILE) + blocks,)),
-                pltpu.SemaphoreType.DMA((N_KINDS, blocks)),
-                pltpu.SemaphoreType.DMA((N_KINDS, blocks)),
+                pltpu.SemaphoreType.DMA((5 + ff // TILE + blocks,)),
+                pltpu.SemaphoreType.DMA((3,)),
+                pltpu.SemaphoreType.DMA((N_RECV, blocks)),
+                pltpu.SemaphoreType.DMA((1,)),
             ],
             compiler_params=pltpu.CompilerParams(
                 collective_id=0, has_side_effects=True, vmem_limit_bytes=52 * 2**20),
             name='layer',
-        )(x_in, g_norm, w_q, w_k, w_v, w_o, w_gate, w_up, w_down, *consts)
+        )(x_in, g_norm, w_q, w_k, w_v, w_o, w_gate, w_up, w_down, rope)
         y_out, k_rot, v_proj = pl.pallas_call(
             store_kernel,
             out_shape=tuple(jax.ShapeDtypeStruct(a.shape, BF16) for a in (y_out, k_rot, v_proj)),

time: 78.1 us -> 72.7 us (0.931)
  Pallas kernels: 77.4 us -> 71.8 us
    pallas_call x1, Pallas kernels: 74.4 us -> 68.9 us  [local_layer(): pl.pallas_call(functools.partial(layer_kernel, n_tp), out_shape=(pltpu.VM...]
where the time goes in v3:
time: 72.7 us
  Pallas kernels  71.8 us (99%)
  between operations  0.82 us (1%)
    pallas_call x1, Pallas kernels, local_layer(): pl.pallas_call(functools.partial(layer_kernel, n_tp), out_shape=(pltpu.VM...  68.9 us
    pallas_call x1, Pallas kernels, local_layer(): pl.pallas_call(store_kernel, out_shape=tuple((jax.ShapeDtypeStruct(a.shap...  2.98 us

profile of v3, /device:TPU:113, one launch (start us, length us, event | category | flops | bytes accessed | tf_op | source)
XLA Modules:
  0.0 72.7 jit_solution(16012423161586923183)
XLA Ops:
  0.6 68.9 %layer.1 = (bf16[1536,2048]{1,0:T(8,128)(2,1)S(1)}, bf16[1536,128]{1,0:T(8,128)(2,1)S(1)}, bf16[1536,128]{1,0:T(8,128)(2,1)S(1)}) custom-call(bf16[1536,2048]{1,0:T(8,128)(2,1)} %x_hbm.1, bf16[2048]{0:T(1024)(128)(2,1)} %g_hbm.1, bf16[2048,256]{1,0:T(8,128)(2,1)} %wq_hbm.1, bf16[2048,1024]{1,0:T(8,128)(2,1)} %wk_hbm.1, bf16[2048,1024]{1,0:T(8,128)(2,1)} %wv_hbm.1, ...), custom_call_target="tpu_custom_call" | custom-call | tf_op jit(solution)/shard_map/layer/pallas_call | solution.py:361
  69.5 3.0 %store.1 = (bf16[1536,2048]{1,0:T(8,128)(2,1)}, bf16[1536,128]{1,0:T(8,128)(2,1)}, bf16[1536,128]{1,0:T(8,128)(2,1)}) custom-call(bf16[1536,2048]{1,0:T(8,128)(2,1)S(1)} %get-tuple-element.9.y_ref, bf16[1536,128]{1,0:T(8,128)(2,1)S(1)} %get-tuple-element.10.k_ref, bf16[1536,128]{1,0:T(8,128)(2,1)S(1)} %get-tuple-element.11.v_ref), custom_call_target="tpu_custom_call" | custom-call | tf_op jit(solution)/shard_map/store/pallas_call | solution.py:396

commit v4 on v3

--- a/solution.py
+++ b/solution.py
@@ -27,35 +27,26 @@
 S_SWAP, S_LINK, S_PARTNER = range(3)
 
 PLACES = {
-    (1, 'project'): (('chip_sum_a', 0),),
-    (1, 'values'): (('chip_sum_b', 0),),
-    (1, 'out1'): (('pass_on_a', 0),),
-    (2, 'start'): (('pass_on_b', 0),),
-    (2, 'project'): (('chip_sum_a', 1),),
-    (2, 'values'): (('chip_sum_b', 1),),
-    (2, 'mlp1'): (('finish', 0),),
-    (2, 'out1'): (('pass_on_a', 1),),
-    (3, 'start'): (('pass_on_b', 1),),
+    (1, 'project'): (('chip_sum_a', 0), ('chip_sum_b', 0),),
+    (1, 'out1'): (('pass_on_a', 0), ('pass_on_b', 0), ('chip_sum_a', 1),),
+    (2, 'project'): (('chip_sum_b', 1),),
+    (2, 'mlp2'): (('finish', 0),),
+    (2, 'out1'): (('pass_on_a', 1), ('pass_on_b', 1), ('chip_sum_b', 2),),
     (3, 'project'): (('chip_sum_a', 2),),
-    (3, 'values'): (('chip_sum_b', 2),),
-    (3, 'mlp1'): (('finish', 1),),
+    (3, 'mlp2'): (('spread', 0), ('finish', 1), ('pass_on_b', 2),),
     (3, 'out1'): (('pass_on_a', 2),),
-    (4, 'start'): (('pass_on_b', 2),),
-    (4, 'project'): (('spread', 0), ('chip_sum_a', 3),),
-    (4, 'values'): (('chip_sum_b', 3),),
-    (4, 'mlp1'): (('finish', 2),),
-    (4, 'out1'): (('far', 0), ('pass_on_a', 3),),
-    (5, 'start'): (('pass_on_b', 3),),
-    (5, 'project'): (('spread', 1), ('chip_sum_a', 4),),
-    (5, 'values'): (('chip_sum_b', 4),),
-    (5, 'mlp1'): (('finish', 3),),
-    (5, 'out1'): (('far', 1), ('pass_on_a', 4),),
+    (4, 'project'): (('chip_sum_a', 3), ('chip_sum_b', 3),),
+    (4, 'out1'): (('finish', 2), ('chip_sum_a', 4),),
+    (5, 'project'): (('spread', 1),),
+    (5, 'mlp2'): (('spread', 2), ('chip_sum_b', 4),),
+    (5, 'out1'): (('chip_sum_a', 5), ('chip_sum_b', 5),),
 }
 DRAIN = (
-    ('spread', 2), ('chip_sum_a', 5), ('chip_sum_b', 5), ('pass_on_b', 4),
-    ('spread', 3), ('far', 2), ('pass_on_a', 5), ('pass_on_b', 5),
-    ('finish', 4), ('far', 3), ('finish', 5), ('spread', 4),
-    ('spread', 5), ('far', 4), ('far', 5),
+    ('pass_on_a', 3), ('pass_on_a', 4), ('pass_on_b', 3), ('far', 0),
+    ('far', 1), ('far', 2), ('pass_on_b', 4), ('pass_on_a', 5),
+    ('pass_on_b', 5), ('finish', 3), ('finish', 4), ('finish', 5),
+    ('spread', 3), ('spread', 4), ('spread', 5), ('far', 3),
+    ('far', 4), ('far', 5),
 )
 
 
@@ -98,26 +89,19 @@
     kv_col = pl.multiple_of(me * HEAD_DIM, HEAD_DIM)
     def x_load(t):
         rows = pl.ds(pl.multiple_of(t * ROWS, ROWS), ROWS)
-        return pltpu.make_async_copy(x_hbm.at[rows], x_v.at[rows], load_sem.at[5 + ff // TILE + t])
+        return pltpu.make_async_copy(x_hbm.at[rows], x_v.at[rows], load_sem.at[5 + t])
     def load(i, src, dst):
         return pltpu.make_async_copy(src, dst, load_sem.at[i])
     ff_tiles = ff // TILE
-    L_SMALL, L_QKV, L_OUT, L_MLP, L_X = 0, 2, 3, 5, 5 + ff_tiles
+    L_SMALL, L_QKV, L_MLP, L_OUT = 0, 2, 3, 4
     small_loads = [load(L_SMALL, g_hbm, g_v), load(L_SMALL + 1, rope_hbm, rope)]
     qkv_loads = [
         load(L_QKV, wq_hbm, wqkv.at[:, pl.ds(0, qw)]),
         load(L_QKV, wk_hbm.at[:, pl.ds(kv_col, HEAD_DIM)], wqkv.at[:, pl.ds(qw, HEAD_DIM)]),
         load(L_QKV, wv_hbm.at[:, pl.ds(kv_col, HEAD_DIM)], wqkv.at[:, pl.ds(qw + HEAD_DIM, HEAD_DIM)]),
     ]
-    mlp_loads = []
-    for j in range(ff_tiles):
-        cols, up_cols = pl.ds(j * TILE, TILE), pl.ds(ff + j * TILE, TILE)
-        mlp_loads += [load(L_MLP + j, wg_hbm.at[:, cols], wgu.at[:, cols]),
-                      load(L_MLP + j, wu_hbm.at[:, cols], wgu.at[:, up_cols])]
-    out_loads = []
-    for i, cols in enumerate((A, B)):
-        out_loads += [load(L_OUT + i, wo_hbm.at[:, cols], wod.at[pl.ds(0, qw), cols]),
-                      load(L_OUT + i, wd_hbm.at[:, cols], wod.at[pl.ds(qw, ff), cols])]
+    mlp_loads = [load(L_MLP, wg_hbm, wgu.at[:, pl.ds(0, ff)]), load(L_MLP, wu_hbm, wgu.at[:, pl.ds(ff, ff)])]
+    out_loads = [load(L_OUT, wo_hbm, wod.at[pl.ds(0, qw)]), load(L_OUT, wd_hbm, wod.at[pl.ds(qw, ff)])]
     x_load(0).start()
     for cp in small_loads + qkv_loads + mlp_loads + out_loads:
         cp.start()
@@ -171,10 +155,10 @@
     scale = 1.0 / math.sqrt(HEAD_DIM) * math.log2(math.e)
 
     def project(t):
-        x_load(t).wait()
         if t == 0:
             for cp in small_loads:
                 cp.wait()
+        x_load(t).wait()
         step = 64
         gain = g_v[...].astype(F32).reshape(1, width)
         for i in range(ROWS // step):
@@ -242,14 +226,16 @@
             om_s[:, pl.ds(h * HEAD_DIM, HEAD_DIM)] = o_s[pl.ds(h * ROWS, ROWS), :].astype(BF16)
 
     def mlp(t, j):
-        loaded(t, L_MLP + j, wgu.at[:, pl.ds(0, 2 * TILE)])
+        if j == 0:
+            loaded(t, L_MLP, wgu)
         a = a_s[...]
         gate = jnp.dot(a, wgu[:, pl.ds(j * TILE, TILE)], preferred_element_type=F32)
         up = jnp.dot(a, wgu[:, pl.ds(ff + j * TILE, TILE)], preferred_element_type=F32)
         om_s[:, pl.ds(qw + j * TILE, TILE)] = (jax.nn.silu(gate) * up).astype(BF16)
 
     def out_half(t, which, kind):
-        loaded(t, L_OUT + which, wod.at[:, A])
+        if which == 0:
+            loaded(t, L_OUT, wod)
         om = om_s[...]
         rows = pl.ds(pl.multiple_of(t * ROWS, ROWS), ROWS)
         tiles = width // TILE // 2
@@ -305,16 +291,17 @@
             stages[name](t)
 
     def step(s):
+        parts = {'project': lambda: project(s), 'scores': lambda: attend_scores(s), 'values': lambda: attend_values(s)}
+        parts.update(('mlp%d' % j, functools.partial(mlp, s, j)) for j in range(ff_tiles))
+        mlp_parts = ['mlp%d' % j for j in range(ff_tiles)]
+        if s == 0:
+            order = ['project', 'scores', 'values'] + mlp_parts
+        else:
+            order = ['project', mlp_parts[0], 'scores'] + mlp_parts[1:-1] + ['values', mlp_parts[-1]]
         place('start', s)
-        project(s)
-        place('project', s)
-        attend_scores(s)
-        place('scores', s)
-        attend_values(s)
-        place('values', s)
-        for j in range(ff_tiles):
-            mlp(s, j)
-            place('mlp%d' % j, s)
+        for name in order:
+            parts[name]()
+            place(name, s)
         if s == 0:
             pl.semaphore_wait(barrier, 3)
         out_half(s, 0, SWAP_A)
@@ -384,7 +371,7 @@
                 pltpu.VMEM((blocks * chunk, width), BF16),
                 pltpu.VMEM((blocks * chunk, width), BF16),
                 pltpu.VMEM((blocks * chunk, width), BF16),
-                pltpu.SemaphoreType.DMA((5 + ff // TILE + blocks,)),
+                pltpu.SemaphoreType.DMA((5 + blocks,)),
                 pltpu.SemaphoreType.DMA((3,)),
                 pltpu.SemaphoreType.DMA((N_RECV, blocks)),
                 pltpu.SemaphoreType.DMA((1,)),

time: 72.7 us -> 71.4 us (0.982)
  Pallas kernels: 71.8 us -> 70.5 us
    pallas_call x1, Pallas kernels: 68.9 us -> 67.6 us  [local_layer(): pl.pallas_call(functools.partial(layer_kernel, n_tp), out_shape=(pltpu.VM...]
where the time goes in v4:
time: 71.4 us
  Pallas kernels  70.5 us (99%)
  between operations  0.82 us (1%)
    pallas_call x1, Pallas kernels, local_layer(): pl.pallas_call(functools.partial(layer_kernel, n_tp), out_shape=(pltpu.VM...  67.6 us
    pallas_call x1, Pallas kernels, local_layer(): pl.pallas_call(store_kernel, out_shape=tuple((jax.ShapeDtypeStruct(a.shap...  2.98 us

profile of v4, /device:TPU:113, one launch (start us, length us, event | category | flops | bytes accessed | tf_op | source)
XLA Modules:
  0.0 71.4 jit_solution(7596443431058644650)
XLA Ops:
  0.6 67.6 %layer.1 = (bf16[1536,2048]{1,0:T(8,128)(2,1)S(1)}, bf16[1536,128]{1,0:T(8,128)(2,1)S(1)}, bf16[1536,128]{1,0:T(8,128)(2,1)S(1)}) custom-call(bf16[1536,2048]{1,0:T(8,128)(2,1)} %x_hbm.1, bf16[2048]{0:T(1024)(128)(2,1)} %g_hbm.1, bf16[2048,256]{1,0:T(8,128)(2,1)} %wq_hbm.1, bf16[2048,1024]{1,0:T(8,128)(2,1)} %wk_hbm.1, bf16[2048,1024]{1,0:T(8,128)(2,1)} %wv_hbm.1, ...), custom_call_target="tpu_custom_call" | custom-call | tf_op jit(solution)/shard_map/layer/pallas_call | solution.py:348
  68.2 3.0 %store.1 = (bf16[1536,2048]{1,0:T(8,128)(2,1)}, bf16[1536,128]{1,0:T(8,128)(2,1)}, bf16[1536,128]{1,0:T(8,128)(2,1)}) custom-call(bf16[1536,2048]{1,0:T(8,128)(2,1)S(1)} %get-tuple-element.9.y_ref, bf16[1536,128]{1,0:T(8,128)(2,1)S(1)} %get-tuple-element.10.k_ref, bf16[1536,128]{1,0:T(8,128)(2,1)S(1)} %get-tuple-element.11.v_ref), custom_call_target="tpu_custom_call" | custom-call | tf_op jit(solution)/shard_map/store/pallas_call | solution.py:383

commit v5 on v4

--- a/solution.py
+++ b/solution.py
@@ -19,12 +19,17 @@
 MESH = pl.DeviceIdType.MESH
 
 (SWAP_A, SWAP_B, FWD_R, OWN_L, FWD_L, OWN_R, SUM_R, SUM_L, OUT_R, OUT_L, OUT_P, FAR_R, FAR_L,
- P_LEFT, P_RIGHT, P_FAR_A, P_FAR_B) = range(17)
+ P_LEFT, P_RIGHT, P_FAR_A, P_FAR_B,
+ END_R, END_L, END_RP, END_LP, P_END_A, P_END_B,
+ FAR_R_HALF, FAR_L_HALF) = range(25)
 R_SWAP_A, R_SWAP_B, R_FWD_R, R_FWD_L, R_FIN, R_OUT, R_FAR = range(7)
 N_RECV = 7
 ARRIVES = {SWAP_A: R_SWAP_A, SWAP_B: R_SWAP_B, FWD_R: R_FWD_R, FWD_L: R_FWD_L, OWN_L: R_FIN, OWN_R: R_FIN,
-           SUM_R: R_FIN, SUM_L: R_FIN, OUT_R: R_OUT, OUT_L: R_OUT, FAR_R: R_FAR, FAR_L: R_FAR}
+           SUM_R: R_FIN, SUM_L: R_FIN, OUT_R: R_OUT, OUT_L: R_OUT, FAR_R: R_FAR, FAR_L: R_FAR,
+           FAR_R_HALF: R_FAR, FAR_L_HALF: R_FAR}
+TO_PARTNER = (OUT_P, P_LEFT, P_RIGHT, P_FAR_A, P_FAR_B, P_END_A, P_END_B)
 S_SWAP, S_LINK, S_PARTNER = range(3)
+FWD_FIRST = (0,)
 
 PLACES = {
     (1, 'project'): (('chip_sum_a', 0), ('chip_sum_b', 0),),
@@ -83,24 +88,30 @@
     c_o = lax.rem(chip + 2, n_chip)
     right = c_r * 2 + core
     left = c_l * 2 + core
+    right_p, left_p = c_r * 2 + 1 - core, c_l * 2 + 1 - core
 
     A, B = pl.ds(0, wh), pl.ds(wh, wh)
+    A1, A2, B1, B2 = (pl.ds(i * wh // 2, wh // 2) for i in range(4))
 
     kv_col = pl.multiple_of(me * HEAD_DIM, HEAD_DIM)
     def x_load(t):
         rows = pl.ds(pl.multiple_of(t * ROWS, ROWS), ROWS)
-        return pltpu.make_async_copy(x_hbm.at[rows], x_v.at[rows], load_sem.at[5 + t])
+        return pltpu.make_async_copy(x_hbm.at[rows], x_v.at[rows], load_sem.at[4 + ff // TILE + t])
     def load(i, src, dst):
         return pltpu.make_async_copy(src, dst, load_sem.at[i])
     ff_tiles = ff // TILE
-    L_SMALL, L_QKV, L_MLP, L_OUT = 0, 2, 3, 4
+    L_SMALL, L_QKV, L_OUT, L_MLP, L_X = 0, 2, 3, 4, 4 + ff_tiles
     small_loads = [load(L_SMALL, g_hbm, g_v), load(L_SMALL + 1, rope_hbm, rope)]
     qkv_loads = [
         load(L_QKV, wq_hbm, wqkv.at[:, pl.ds(0, qw)]),
         load(L_QKV, wk_hbm.at[:, pl.ds(kv_col, HEAD_DIM)], wqkv.at[:, pl.ds(qw, HEAD_DIM)]),
         load(L_QKV, wv_hbm.at[:, pl.ds(kv_col, HEAD_DIM)], wqkv.at[:, pl.ds(qw + HEAD_DIM, HEAD_DIM)]),
     ]
-    mlp_loads = [load(L_MLP, wg_hbm, wgu.at[:, pl.ds(0, ff)]), load(L_MLP, wu_hbm, wgu.at[:, pl.ds(ff, ff)])]
+    mlp_loads = []
+    for j in range(ff_tiles):
+        cols, up_cols = pl.ds(j * TILE, TILE), pl.ds(ff + j * TILE, TILE)
+        mlp_loads += [load(L_MLP + j, wg_hbm.at[:, cols], wgu.at[:, cols]),
+                      load(L_MLP + j, wu_hbm.at[:, cols], wgu.at[:, up_cols])]
     out_loads = [load(L_OUT, wo_hbm, wod.at[pl.ds(0, qw)]), load(L_OUT, wd_hbm, wod.at[pl.ds(qw, ff)])]
     x_load(0).start()
     for cp in small_loads + qkv_loads + mlp_loads + out_loads:
@@ -113,7 +124,7 @@
             load(sem, ref, ref).wait()
 
     barrier = pltpu.get_barrier_semaphore()
-    for dev in (partner, left, right):
+    for dev in (partner, left, right, left_p, right_p):
         pl.semaphore_signal(barrier, inc=1, device_id={'tp': dev}, device_id_type=MESH)
     def rows_of(t, c):
         return pl.ds(pl.multiple_of(t * ROWS + core * half + c * chunk, chunk), chunk)
@@ -123,6 +134,8 @@
 
     def copy(kind, t):
         other = pl.ds(pl.multiple_of(t * ROWS + (1 - core) * half, half), half)
+        def y_copy(c, cols, dev):
+            return y_ref.at[rows_of(t, c), cols], y_ref.at[rows_of(t, c), cols], dev
         src, dst, dev = {
             SWAP_A: lambda: (part.at[other, A], swap.at[pl.ds(pl.multiple_of(t * half, half), half), A], partner),
             SWAP_B: lambda: (part.at[other, B], swap.at[pl.ds(pl.multiple_of(t * half, half), half), B], partner),
@@ -141,8 +154,16 @@
             P_RIGHT: lambda: (y_ref.at[rows_of(t, c_r)], y_ref.at[rows_of(t, c_r)], partner),
             P_FAR_A: lambda: (y_ref.at[rows_of(t, c_o), A], y_ref.at[rows_of(t, c_o), A], partner),
             P_FAR_B: lambda: (y_ref.at[rows_of(t, c_o), B], y_ref.at[rows_of(t, c_o), B], partner),
+            FAR_R_HALF: lambda: y_copy(c_l, A1, right),
+            FAR_L_HALF: lambda: y_copy(c_r, B1, left),
+            END_R: lambda: y_copy(c_l, A2, right),
+            END_L: lambda: y_copy(c_r, B2, left),
+            END_RP: lambda: y_copy(c_l, A2, right_p),
+            END_LP: lambda: y_copy(c_r, B2, left_p),
+            P_END_A: lambda: y_copy(c_o, A1, partner),
+            P_END_B: lambda: y_copy(c_o, B1, partner),
         }[kind]()
-        leaves = S_SWAP if kind in (SWAP_A, SWAP_B) else S_LINK if kind in ARRIVES else S_PARTNER
+        leaves = S_SWAP if kind in (SWAP_A, SWAP_B) else S_PARTNER if kind in TO_PARTNER else S_LINK
         return pltpu.make_async_remote_copy(
             src_ref=src, dst_ref=dst, send_sem=send_sem.at[leaves],
             recv_sem=recv_sem.at[ARRIVES[kind], t] if kind in ARRIVES else done_sem.at[0],
@@ -226,8 +247,7 @@
             om_s[:, pl.ds(h * HEAD_DIM, HEAD_DIM)] = o_s[pl.ds(h * ROWS, ROWS), :].astype(BF16)
 
     def mlp(t, j):
-        if j == 0:
-            loaded(t, L_MLP, wgu)
+        loaded(t, L_MLP + j, wgu.at[:, pl.ds(0, 2 * TILE)])
         a = a_s[...]
         gate = jnp.dot(a, wgu[:, pl.ds(j * TILE, TILE)], preferred_element_type=F32)
         up = jnp.dot(a, wgu[:, pl.ds(ff + j * TILE, TILE)], preferred_element_type=F32)
@@ -268,19 +288,22 @@
         for kind in (OUT_R, OUT_L, OUT_P):
             copy(kind, t).start()
 
+    last = blocks - 1
+
     def spread(t):
         take(recv_sem.at[R_OUT, t], 2 * chunk)
-        for kind in (FAR_R, FAR_L, P_LEFT, P_RIGHT):
+        far_kinds = (FAR_R, FAR_L) if t < last else (FAR_R_HALF, FAR_L_HALF, END_RP, END_LP, END_R, END_L)
+        for kind in far_kinds + (P_LEFT, P_RIGHT):
             copy(kind, t).start()
 
     def far(t):
-        take(recv_sem.at[R_FAR, t], chunk)
-        for kind in (P_FAR_A, P_FAR_B):
+        take(recv_sem.at[R_FAR, t], chunk if t < last else chunk // 2)
+        for kind in (P_FAR_A, P_FAR_B) if t < last else (P_END_A, P_END_B):
             copy(kind, t).start()
 
     stages = {
-        'chip_sum_a': lambda t: chip_sum(t, A, SWAP_A, FWD_R, OWN_L),
-        'chip_sum_b': lambda t: chip_sum(t, B, SWAP_B, FWD_L, OWN_R),
+        'chip_sum_a': lambda t: chip_sum(t, A, SWAP_A, *((FWD_R,) if t in FWD_FIRST else (FWD_R, OWN_L))),
+        'chip_sum_b': lambda t: chip_sum(t, B, SWAP_B, *((FWD_L, OWN_R, OWN_L) if t in FWD_FIRST else (FWD_L, OWN_R))),
         'pass_on_a': lambda t: pass_on(t, A, FWD_R, SUM_R, c_r),
         'pass_on_b': lambda t: pass_on(t, B, FWD_L, SUM_L, c_l),
         'finish': finish, 'spread': spread, 'far': far,
@@ -294,16 +317,13 @@
         parts = {'project': lambda: project(s), 'scores': lambda: attend_scores(s), 'values': lambda: attend_values(s)}
         parts.update(('mlp%d' % j, functools.partial(mlp, s, j)) for j in range(ff_tiles))
         mlp_parts = ['mlp%d' % j for j in range(ff_tiles)]
-        if s == 0:
-            order = ['project', 'scores', 'values'] + mlp_parts
-        else:
-            order = ['project', mlp_parts[0], 'scores'] + mlp_parts[1:-1] + ['values', mlp_parts[-1]]
+        order = ['project', mlp_parts[0], 'scores'] + mlp_parts[1:-1] + ['values', mlp_parts[-1]]
         place('start', s)
         for name in order:
             parts[name]()
             place(name, s)
         if s == 0:
-            pl.semaphore_wait(barrier, 3)
+            pl.semaphore_wait(barrier, 5)
         out_half(s, 0, SWAP_A)
         place('out0', s)
         out_half(s, 1, SWAP_B)
@@ -313,10 +333,10 @@
         step(s)
     for name, t in DRAIN:
         stages[name](t)
-    take(done_sem.at[0], tokens // 2)
+    take(done_sem.at[0], tokens // 2 + chunk // 2)
     take(send_sem.at[S_SWAP], tokens // 2)
-    take(send_sem.at[S_LINK], tokens * 3 // 4)
-    take(send_sem.at[S_PARTNER], tokens // 2)
+    take(send_sem.at[S_LINK], tokens * 3 // 4 + chunk // 2)
+    take(send_sem.at[S_PARTNER], tokens // 2 - chunk // 2)
 
 
 def store_kernel(y_ref, k_ref, v_ref, y_hbm, k_hbm, v_hbm, sem):
@@ -371,7 +391,7 @@
                 pltpu.VMEM((blocks * chunk, width), BF16),
                 pltpu.VMEM((blocks * chunk, width), BF16),
                 pltpu.VMEM((blocks * chunk, width), BF16),
-                pltpu.SemaphoreType.DMA((5 + blocks,)),
+                pltpu.SemaphoreType.DMA((4 + ff // TILE + blocks,)),
                 pltpu.SemaphoreType.DMA((3,)),
                 pltpu.SemaphoreType.DMA((N_RECV, blocks)),
                 pltpu.SemaphoreType.DMA((1,)),

time: 71.4 us -> 70.9 us (level)
  no operation moved by 1% of the time
where the time goes in v5:
time: 70.9 us; the launch traced here: 70.8 us
  Pallas kernels  70 us (99%)
  between operations  0.82 us (1%)
    pallas_call x1, Pallas kernels, local_layer(): pl.pallas_call(functools.partial(layer_kernel, n_tp), out_shape=(pltpu.VM...  67 us
    pallas_call x1, Pallas kernels, local_layer(): pl.pallas_call(store_kernel, out_shape=tuple((jax.ShapeDtypeStruct(a.shap...  2.98 us

profile of v5, /device:TPU:113, one launch (start us, length us, event | category | flops | bytes accessed | tf_op | source)
XLA Modules:
  0.0 70.8 jit_solution(8630555447439014312)
XLA Ops:
  0.6 67.0 %layer.1 = (bf16[1536,2048]{1,0:T(8,128)(2,1)S(1)}, bf16[1536,128]{1,0:T(8,128)(2,1)S(1)}, bf16[1536,128]{1,0:T(8,128)(2,1)S(1)}) custom-call(bf16[1536,2048]{1,0:T(8,128)(2,1)} %x_hbm.1, bf16[2048]{0:T(1024)(128)(2,1)} %g_hbm.1, bf16[2048,256]{1,0:T(8,128)(2,1)} %wq_hbm.1, bf16[2048,1024]{1,0:T(8,128)(2,1)} %wk_hbm.1, bf16[2048,1024]{1,0:T(8,128)(2,1)} %wv_hbm.1, ...), custom_call_target="tpu_custom_call" | custom-call | tf_op jit(solution)/shard_map/layer/pallas_call | solution.py:368
  67.6 3.0 %store.1 = (bf16[1536,2048]{1,0:T(8,128)(2,1)}, bf16[1536,128]{1,0:T(8,128)(2,1)}, bf16[1536,128]{1,0:T(8,128)(2,1)}) custom-call(bf16[1536,2048]{1,0:T(8,128)(2,1)S(1)} %get-tuple-element.9.y_ref, bf16[1536,128]{1,0:T(8,128)(2,1)S(1)} %get-tuple-element.10.k_ref, bf16[1536,128]{1,0:T(8,128)(2,1)S(1)} %get-tuple-element.11.v_ref), custom_call_target="tpu_custom_call" | custom-call | tf_op jit(solution)/shard_map/store/pallas_call | solution.py:403

commit v6 on v5

--- a/solution.py
+++ b/solution.py
@@ -13,7 +13,7 @@
 NORM_EPS = 1e-5
 ROWS = 256
 TILE = 256
-STORES = 8
+STORES = 1
 F32 = jnp.float32
 BF16 = jnp.bfloat16
 MESH = pl.DeviceIdType.MESH
@@ -38,8 +38,8 @@
     (2, 'mlp2'): (('finish', 0),),
     (2, 'out1'): (('pass_on_a', 1), ('pass_on_b', 1), ('chip_sum_b', 2),),
     (3, 'project'): (('chip_sum_a', 2),),
-    (3, 'mlp2'): (('spread', 0), ('finish', 1), ('pass_on_b', 2),),
-    (3, 'out1'): (('pass_on_a', 2),),
+    (3, 'mlp2'): (('spread', 0), ('finish', 1),),
+    (3, 'out1'): (('pass_on_b', 2), ('pass_on_a', 2),),
     (4, 'project'): (('chip_sum_a', 3), ('chip_sum_b', 3),),
     (4, 'out1'): (('finish', 2), ('chip_sum_a', 4),),
     (5, 'project'): (('spread', 1),),

time: 70.9 us -> 70.9 us (level)
  no operation moved by 1% of the time
where the time goes in v6:
time: 70.9 us; the launch traced here: 70.8 us
  Pallas kernels  70 us (99%)
  between operations  0.82 us (1%)
    pallas_call x1, Pallas kernels, local_layer(): pl.pallas_call(functools.partial(layer_kernel, n_tp), out_shape=(pltpu.VM...  67 us
    pallas_call x1, Pallas kernels, local_layer(): pl.pallas_call(store_kernel, out_shape=tuple((jax.ShapeDtypeStruct(a.shap...  2.96 us

profile of v6, /device:TPU:113, one launch (start us, length us, event | category | flops | bytes accessed | tf_op | source)
XLA Modules:
  0.0 70.8 jit_solution(6074793566977187934)
XLA Ops:
  0.6 67.0 %layer.1 = (bf16[1536,2048]{1,0:T(8,128)(2,1)S(1)}, bf16[1536,128]{1,0:T(8,128)(2,1)S(1)}, bf16[1536,128]{1,0:T(8,128)(2,1)S(1)}) custom-call(bf16[1536,2048]{1,0:T(8,128)(2,1)} %x_hbm.1, bf16[2048]{0:T(1024)(128)(2,1)} %g_hbm.1, bf16[2048,256]{1,0:T(8,128)(2,1)} %wq_hbm.1, bf16[2048,1024]{1,0:T(8,128)(2,1)} %wk_hbm.1, bf16[2048,1024]{1,0:T(8,128)(2,1)} %wv_hbm.1, ...), custom_call_target="tpu_custom_call" | custom-call | tf_op jit(solution)/shard_map/layer/pallas_call | solution.py:368
  67.6 3.0 %store.1 = (bf16[1536,2048]{1,0:T(8,128)(2,1)}, bf16[1536,128]{1,0:T(8,128)(2,1)}, bf16[1536,128]{1,0:T(8,128)(2,1)}) custom-call(bf16[1536,2048]{1,0:T(8,128)(2,1)S(1)} %get-tuple-element.9.y_ref, bf16[1536,128]{1,0:T(8,128)(2,1)S(1)} %get-tuple-element.10.k_ref, bf16[1536,128]{1,0:T(8,128)(2,1)S(1)} %get-tuple-element.11.v_ref), custom_call_target="tpu_custom_call" | custom-call | tf_op jit(solution)/shard_map/store/pallas_call | solution.py:403
